TPU v7x, 32 devices: a whole 2x2x4 slice. The times are simulated.
32 devices in a mesh: dom: 32 (over z, y, x, core).
Axes of the slice: x: 2, y: 2, z: 4, core: 2. Of those that a mesh axis runs over, the one named last changes fastest.
Arguments:
- features: bfloat16 [131072, 256], P('dom'), may hold values from -6 to 6
- weight: bfloat16 [256, 256], replicated, may hold values from -0.375 to 0.375
- bias_vector: float32 [256], replicated, may hold values from -3 to 3
- tile_values: bfloat16 [8192, 128, 128], P('dom'), may hold values from -0.1875 to 0.1875
- tile_row: int32 [32, 256], P('dom'), may hold values from 0 to 31
- tile_col: int32 [32, 256], P('dom'), may hold values from 0 to 35
- tile_count: int32 [32], P('dom'), may hold values from 64 to 256, as said below
- send_rows: int32 [32, 32, 16], P('dom'), may hold values from 0 to 4095, as said below
- send_count: int32 [32, 32], P('dom'), may hold values from 0 to 16, as said below
- cotangent: bfloat16 [131072, 256], P('dom'), may hold values from -6 to 6
Outputs:
- activation: bfloat16 [131072, 256], P('dom')
- grad_features: bfloat16 [131072, 256], P('dom')
- grad_weight: float32 [256, 256], replicated
- grad_bias: float32 [256], replicated
Inputs may be any that keep to these rules, and one draw needn't show every extreme that they name: `tile_count`: each partition uses at least a quarter of its slots; in every draw two partitions use all 256. `send_rows`: for each sender and reader the 16 listed rows are distinct. `send_count`: in every draw one reader receives 16 rows from every partition.
All inputs are finite; a program needn't handle non-finite values.
Results may differ from a plain program's by a relative error of at most 0.0061.
Values may be sent and summed in bfloat16 or wider, within the bound.
A program may use at most 192 MiB of HBM per device.

v0:
```python
import functools
import math

import jax
import jax.numpy as jnp
from jax import lax
from jax.experimental import pallas as pl
from jax.experimental.pallas import tpu as pltpu
from jax.sharding import PartitionSpec as P

MESH = pl.DeviceIdType.MESH
VMEM = pltpu.VMEM
f32 = jnp.float32
bf16 = jnp.bfloat16


def greet(n, me):
    barrier = pltpu.get_barrier_semaphore()

    def signal(i, carry):
        pl.semaphore_signal(
            barrier, inc=1, device_id=(lax.rem(me + i, n),), device_id_type=MESH
        )
        return carry

    lax.fori_loop(1, n, signal, 0)
    return barrier


def push(n, me, src, dst, send_sem, recv_sem, i):
    peer = lax.rem(me + i, n)
    return pltpu.make_async_remote_copy(
        src_ref=src(peer),
        dst_ref=dst.at[me],
        send_sem=send_sem.at[i],
        recv_sem=recv_sem.at[i],
        device_id=(peer,),
        device_id_type=MESH,
    )


def live(count_ref, peer, values):
    slot = lax.broadcasted_iota(jnp.int32, values.shape, 0)
    return jnp.where(slot < count_ref[0, peer], values, jnp.zeros_like(values))


def gather_kernel(
    n, count_ref, chosen_ref, features_hbm, halo_ref,
    features_ref, total, sent, landed, send_sem, recv_sem, load_sem,
):
    me = lax.axis_index("dom")
    slots = chosen_ref.shape[0]
    rows = features_ref.shape[0]
    step = math.gcd(rows, 512)
    loads = []
    for c in range(rows // step):
        span = pl.ds(c * step, step)
        loads.append(
            pltpu.make_async_copy(features_hbm.at[span], features_ref.at[span], load_sem.at[c])
        )
        loads[c].start()
    barrier = greet(n, me)
    for c in range(rows // step):
        ids = lax.broadcasted_iota(jnp.int32, (slots, step), 1) + c * step
        hot = jnp.where(ids == chosen_ref[...], 1.0, 0.0).astype(bf16)
        loads[c].wait()
        part = jnp.dot(hot, features_ref[pl.ds(c * step, step), :], preferred_element_type=f32)
        if c == 0:
            total[...] = part
        else:
            total[...] += part
    slot_count = sent.shape[1]
    for p in range(n):
        block = total[pl.ds(p * slot_count, slot_count), :]
        sent[p] = live(count_ref, p, block).astype(bf16)
    pl.semaphore_wait(barrier, n - 1)
    copy = functools.partial(push, n, me, lambda p: sent.at[p], landed, send_sem, recv_sem)

    def start(i, carry):
        copy(i).start()
        return carry

    def finish(i, carry):
        copy(i).wait()
        return carry

    lax.fori_loop(1, n, start, 0)
    landed[me] = sent[me]
    lax.fori_loop(1, n, finish, 0)
    halo_ref[...] = landed[...]


def exchange_gather(n, send_count, chosen, features, slot_count):
    width = features.shape[1]
    slots = chosen.shape[0]
    block = (n, slot_count, width)
    return pl.pallas_call(
        functools.partial(gather_kernel, n),
        out_shape=jax.ShapeDtypeStruct(block, bf16),
        in_specs=[
            pl.BlockSpec(memory_space=pltpu.SMEM),
            pl.BlockSpec(memory_space=VMEM),
            pl.BlockSpec(memory_space=pltpu.HBM),
        ],
        out_specs=pl.BlockSpec(memory_space=VMEM),
        scratch_shapes=[
            VMEM(features.shape, bf16),
            VMEM((slots, width), f32),
            VMEM(block, bf16),
            VMEM(block, bf16),
            pltpu.SemaphoreType.DMA((n,)),
            pltpu.SemaphoreType.DMA((n,)),
            pltpu.SemaphoreType.DMA((features.shape[0] // math.gcd(features.shape[0], 512),)),
        ],
        compiler_params=pltpu.CompilerParams(
            collective_id=0, has_side_effects=True, vmem_limit_bytes=60 * 1024 * 1024
        ),
        cost_estimate=pl.CostEstimate(
            flops=2 * slots * features.shape[0] * width,
            bytes_accessed=16 * features.size,
            transcendentals=0,
        ),
        name="gather_exchange",
    )(send_count, chosen, features)


GROUP = 8
CHUNK = 16


def local_kernel(
    tile_row, tile_col, tile_count, features, halo, tiles, cotangent, weight, bias,
    activation, own_grad, halo_grad, weight_part, bias_part,
    source, held, cot, act, mixed, forward, backward, spread, wsum, bsum,
    in_sem, tile_sem, cot_sem, act_sem, out_sem,
):
    own = features.shape[0]
    ext = own + halo.shape[0]
    number = tiles.shape[0]
    chunk = math.gcd(number, CHUNK)
    group = math.gcd(chunk, GROUP)
    total = tile_count[0]
    chunks = (total + chunk - 1) // chunk

    def tile_copy(c):
        span = pl.ds(c * chunk, chunk)
        return pltpu.make_async_copy(tiles.at[span], held.at[span], tile_sem.at[c])

    copies = [
        pltpu.make_async_copy(features, source.at[pl.ds(0, own)], in_sem.at[0]),
        pltpu.make_async_copy(halo, source.at[pl.ds(own, ext - own)], in_sem.at[1]),
    ]
    for copy in copies:
        copy.start()

    @pl.loop(0, chunks)
    def _(c):
        tile_copy(c).start()

    cot_copy = pltpu.make_async_copy(cotangent, cot, cot_sem)
    cot_copy.start()

    @pl.loop(0, own)
    def _(r):
        forward[r] = jnp.zeros(forward.shape[1:], f32)
        backward[r] = jnp.zeros(backward.shape[1:], f32)

    for r in range(own, ext):
        backward[r] = jnp.zeros(backward.shape[1:], f32)
    for copy in copies:
        copy.wait()

    @pl.loop(0, chunks)
    def _(c):
        tile_copy(c).wait()
        for g in range(chunk // group):
            base = c * chunk + g * group
            for j in range(group):
                k = base + j
                product = jnp.dot(held[k], source[tile_col[0, k]], preferred_element_type=f32)
                target = jnp.where(k < total, tile_row[0, k], own)
                forward[target] += product

    cot_copy.wait()
    edge = tiles.shape[1]
    step = math.gcd(own, 4)
    width = weight.shape[0]
    wsum[...] = jnp.zeros_like(wsum)
    bsum[...] = jnp.zeros_like(bsum)

    def act_copy(b):
        span = pl.ds(b * step, step)
        return pltpu.make_async_copy(act.at[span], activation.at[span], act_sem.at[b])

    @pl.loop(0, own // step)
    def _(b):
        span = pl.ds(b * step, step)
        agg = forward[span].astype(bf16).reshape(step * edge, width)
        linear = jnp.dot(agg, weight[...], preferred_element_type=f32) + bias[...]
        sig = jax.nn.sigmoid(linear)
        act[span] = (linear * sig).astype(bf16).reshape(step, edge, width)
        act_copy(b).start()
        slope = sig * (1.0 + linear * (1.0 - sig))
        grad = (cot[span].reshape(step * edge, width).astype(f32) * slope).astype(bf16)
        wsum[...] += lax.dot_general(
            agg, grad, (((0,), (0,)), ((), ())), preferred_element_type=f32
        )
        bsum[...] += jnp.sum(grad.astype(f32), axis=0, keepdims=True)
        back = lax.dot_general(
            grad, weight[...], (((1,), (1,)), ((), ())), preferred_element_type=f32
        )
        mixed[span] = back.astype(bf16).reshape(step, edge, width)

    @pl.loop(0, chunks * (chunk // group))
    def _(g):
        for j in range(group):
            k = g * group + j
            product = lax.dot_general(
                held[k], mixed[tile_row[0, k]], (((0,), (0,)), ((), ())),
                preferred_element_type=f32,
            )
            target = jnp.where(k < total, tile_col[0, k], ext)
            backward[target] += product

    def out_copy(b):
        span = pl.ds(b * step, step)
        return pltpu.make_async_copy(spread.at[span], own_grad.at[span], out_sem.at[b])

    @pl.loop(0, own // step)
    def _(b):
        span = pl.ds(b * step, step)
        spread[span] = backward[span].astype(bf16)
        out_copy(b).start()

    halo_grad[...] = backward[pl.ds(own, ext - own)].astype(bf16)
    pieces, piece_rows = weight_part.shape[:2]
    for p in range(pieces):
        weight_part[p] = wsum[pl.ds(p * piece_rows, piece_rows), :].astype(bf16)
    bias_part[...] = bsum[...]

    @pl.loop(0, own // step)
    def _(b):
        act_copy(b).wait()
        out_copy(b).wait()


def local_pass(n, tile_row, tile_col, tile_count, features, halo, tiles, cotangent, weight, bias):
    own, edge, width = features.shape
    ext = own + halo.shape[0]
    number = tiles.shape[0]
    chunk = math.gcd(number, CHUNK)
    steps = own // math.gcd(own, 4)
    anywhere = pl.BlockSpec(memory_space=pltpu.HBM)
    smem = pl.BlockSpec(memory_space=pltpu.SMEM)
    vmem = pl.BlockSpec(memory_space=VMEM)
    dma = pltpu.SemaphoreType.DMA
    return pl.pallas_call(
        local_kernel,
        out_shape=(
            jax.ShapeDtypeStruct(features.shape, bf16),
            jax.ShapeDtypeStruct(features.shape, bf16),
            jax.ShapeDtypeStruct(halo.shape, bf16),
            jax.ShapeDtypeStruct((n, width // n, width), bf16),
            jax.ShapeDtypeStruct((1, width), f32),
        ),
        in_specs=[smem] * 3 + [anywhere] * 4 + [vmem] * 2,
        out_specs=(anywhere, anywhere, vmem, vmem, vmem),
        scratch_shapes=[
            VMEM((ext, edge, width), bf16),
            VMEM(tiles.shape, bf16),
            VMEM(features.shape, bf16),
            VMEM(features.shape, bf16),
            VMEM(features.shape, bf16),
            VMEM((own + 1, edge, width), f32),
            VMEM((ext + 1, edge, width), f32),
            VMEM(features.shape, bf16),
            VMEM((width, width), f32),
            VMEM((1, width), f32),
            dma((2,)),
            dma((number // chunk,)),
            dma,
            dma((steps,)),
            dma((steps,)),
        ],
        compiler_params=pltpu.CompilerParams(vmem_limit_bytes=56 * 1024 * 1024),
        name="local_pass",
    )(tile_row, tile_col, tile_count, features, halo, tiles, cotangent, weight, bias)


def return_kernel(
    n, scale, count_ref, chosen_ref, halo_ref, weight_ref, bias_ref, own_hbm,
    out_hbm, wsum_ref, bsum_ref,
    halo_in, weight_in, bias_in, piece, pieces_in, returned, own, hot, out, load_sem, out_sem,
    halo_s, halo_r, weight_s, weight_r, bias_s, bias_r, piece_s, piece_r,
):
    me = lax.axis_index("dom")
    load = pltpu.make_async_copy(own_hbm, own, load_sem)
    load.start()
    barrier = greet(n, me)
    pl.semaphore_wait(barrier, n - 1)
    halo_copy = functools.partial(push, n, me, lambda p: halo_ref.at[p], halo_in, halo_s, halo_r)
    weight_copy = functools.partial(
        push, n, me, lambda p: weight_ref.at[p], weight_in, weight_s, weight_r
    )
    bias_copy = functools.partial(push, n, me, lambda p: bias_ref, bias_in, bias_s, bias_r)
    piece_copy = functools.partial(push, n, me, lambda p: piece, pieces_in, piece_s, piece_r)

    def over(step):
        def turn(i, carry):
            step(i)
            return carry

        lax.fori_loop(1, n, turn, 0)

    def first(i):
        weight_copy(i).start()
        bias_copy(i).start()

    over(first)
    over(lambda i: halo_copy(i).start())
    weight_in[me] = weight_ref[me]
    bias_in[me] = bias_ref[...]
    halo_in[me] = halo_ref[me]
    rows = own.shape[0]
    slots = chosen_ref.shape[1]
    step = math.gcd(rows, 512)
    for c in range(rows // step):
        ids = lax.broadcasted_iota(jnp.int32, (step, slots), 0) + c * step
        hot[pl.ds(c * step, step), :] = jnp.where(ids == chosen_ref[...], 1.0, 0.0).astype(bf16)
    over(lambda i: weight_copy(i).wait())
    piece[...] = (jnp.sum(weight_in[...].astype(f32), axis=0) * scale).astype(bf16)
    over(lambda i: piece_copy(i).start())
    pieces_in[me] = piece[...]
    over(lambda i: bias_copy(i).wait())
    bsum_ref[...] = jnp.sum(bias_in[...], axis=0) * scale
    over(lambda i: halo_copy(i).wait())
    slot_count = halo_in.shape[1]
    for p in range(n):
        returned[pl.ds(p * slot_count, slot_count), :] = live(
            count_ref, p, halo_in[p].astype(f32)
        ).astype(bf16)
    load.wait()
    outs = []
    for c in range(rows // step):
        span = pl.ds(c * step, step)
        collected = jnp.dot(hot[span, :], returned[...], preferred_element_type=f32)
        out[span, :] = (own[span, :].astype(f32) + collected).astype(bf16)
        outs.append(pltpu.make_async_copy(out.at[span], out_hbm.at[span], out_sem.at[c]))
        outs[c].start()
    over(lambda i: piece_copy(i).wait())
    piece_rows = piece.shape[0]
    for p in range(n):
        wsum_ref[pl.ds(p * piece_rows, piece_rows), :] = pieces_in[p].astype(f32)
    for copy in outs:
        copy.wait()


def exchange_return(n, scale, send_count, chosen, halo_grad, weight_part, bias_part, own_grad):
    rows, width = own_grad.shape
    slots = chosen.shape[1]
    vmem = pl.BlockSpec(memory_space=VMEM)
    hbm = pl.BlockSpec(memory_space=pltpu.HBM)
    return pl.pallas_call(
        functools.partial(return_kernel, n, scale),
        out_shape=(
            jax.ShapeDtypeStruct(own_grad.shape, bf16),
            jax.ShapeDtypeStruct((width, width), f32),
            jax.ShapeDtypeStruct((1, width), f32),
        ),
        in_specs=[pl.BlockSpec(memory_space=pltpu.SMEM)] + [vmem] * 4 + [hbm],
        out_specs=(hbm, vmem, vmem),
        scratch_shapes=[
            VMEM(halo_grad.shape, bf16),
            VMEM(weight_part.shape, bf16),
            VMEM((n,) + bias_part.shape, f32),
            VMEM(weight_part.shape[1:], bf16),
            VMEM(weight_part.shape, bf16),
            VMEM((slots, width), bf16),
            VMEM(own_grad.shape, bf16),
            VMEM((rows, slots), bf16),
            VMEM(own_grad.shape, bf16),
            pltpu.SemaphoreType.DMA,
            pltpu.SemaphoreType.DMA((rows // math.gcd(rows, 512),)),
        ]
        + [pltpu.SemaphoreType.DMA((n,))] * 8,
        compiler_params=pltpu.CompilerParams(
            collective_id=1, has_side_effects=True, vmem_limit_bytes=60 * 1024 * 1024
        ),
        name="return_exchange",
    )(send_count, chosen, halo_grad, weight_part, bias_part, own_grad)


def body(
    features, weight, bias_vector, tile_values, tile_row, tile_col, tile_count, send_rows,
    send_count, cotangent,
):
    rows, width = features.shape
    n = lax.axis_size("dom")
    slot_count = send_rows.shape[2]
    edge = tile_values.shape[1]
    own = rows // edge
    slots = n * slot_count
    halo = exchange_gather(n, send_count, send_rows.reshape(slots, 1), features, slot_count)
    blocks = lambda a: a.reshape(-1, edge, width)
    activation, own_grad, halo_grad, weight_part, bias_part = local_pass(
        n, tile_row, tile_col, tile_count, blocks(features), blocks(halo), tile_values,
        blocks(cotangent), weight, bias_vector.reshape(1, width),
    )
    scale = float(rows * n) ** (-0.5)
    grad_features, weight_sum, bias_sum = exchange_return(
        n, scale, send_count, send_rows.reshape(1, slots),
        halo_grad.reshape(n, slot_count, width), weight_part, bias_part,
        own_grad.reshape(rows, width),
    )
    return (activation.reshape(rows, width), grad_features, weight_sum, bias_sum.reshape(width))


def solution(mesh):
    return jax.shard_map(
        body,
        mesh=mesh,
        in_specs=(
            P("dom", None),
            P(),
            P(),
            P("dom", None, None),
            P("dom", None),
            P("dom", None),
            P("dom"),
            P("dom", None, None),
            P("dom", None),
            P("dom", None),
        ),
        out_specs=(P("dom", None), P("dom", None), P(), P()),
        check_vma=False,
    )
```

profile of v0, /device:TPU:0, one launch (start us, length us, event | category | flops | bytes accessed | tf_op | source)
XLA Modules:
  0.0 72.7 jit_solution(14751319508286815776)
XLA Ops:
  1.3 0.8 %copy.16 = s32[1,32,16]{2,1,0:T(8,128)S(1)} copy(s32[1,32,16]{1,2,0:T(8,128)} %param.17) | data formatting | bytes 4096 | tf_op args[7]
  2.0 0.7 reshape.44.chosen_ref
  2.7 0.9 %reshape.48.chosen_ref = s32[512,1]{1,0:T(8,128)} reshape(s32[1,32,16]{2,1,0:T(8,128)S(1)} %copy.16) | data formatting | bytes 4096 | tf_op jit(solution)/shard_map/reshape | solution.py:403
  3.6 15.9 %gather_exchange.1 = bf16[32,16,256]{2,1,0:T(8,128)(2,1)} custom-call(s32[1,32]{1,0:T(1,128)} %count_ref.3, s32[512,1]{1,0:T(8,128)} %reshape.48.chosen_ref, bf16[4096,256]{1,0:T(8,128)(2,1)} %features_hbm.1), custom_call_target="tpu_custom_call" | custom-call | flops 1073741824 | bytes 16777216 | tf_op jit(solution)/shard_map/gather_exchange/pallas_call | solution.py:97
  19.5 15.3 %local_pass.1 = (bf16[32,128,256]{2,1,0:T(8,128)(2,1)}, bf16[32,128,256]{2,1,0:T(8,128)(2,1)}, bf16[4,128,256]{2,1,0:T(8,128)(2,1)}, bf16[32,8,256]{2,1,0:T(8,128)(2,1)}, f32[1,256]{1,0:T(1,128)}) custom-call(s32[1,256]{1,0:T(1,128)} %tile_row.1, s32[1,256]{1,0:T(1,128)} %tile_col.1, s32[1]{0:T(128)S(6)} %copy.22.tile_count, bf16[32,128,256]{2,1,0:T(8,128)(2,1)} %bitcast.9, ...), custom_call_target="tpu_custom_call" | custom-call | tf_op jit(solution)/shard_map/local_pass/pallas_call | solution.py:257
  34.8 33.6 %return_exchange.1 = (bf16[4096,256]{1,0:T(8,128)(2,1)}, f32[256,256]{1,0:T(8,128)}, f32[1,256]{1,0:T(1,128)}) custom-call(s32[1,32]{1,0:T(1,128)} %count_ref.3, s32[1,512]{1,0:T(1,128)} %reshape.44.chosen_ref, bf16[32,16,256]{2,1,0:T(8,128)(2,1)} %bitcast.11, bf16[32,8,256]{2,1,0:T(8,128)(2,1)} %get-tuple-element.14.weight_ref, ...), custom_call_target="tpu_custom_call" | custom-call | tf_op jit(solution)/shard_map/return_exchange/pallas_call | solution.py:363
  68.4 0.0 copy-start
  68.4 0.0 copy-start.1
  68.4 3.1 %copy.23 = bf16[4096,256]{1,0:T(8,128)(2,1)} copy(bf16[4096,256]{1,0:T(8,128)(2,1)} %get-tuple-element.25) | data formatting | bytes 4194304
  71.5 0.0 copy-done
  71.5 0.7 copy.24
  72.2 0.0 copy-done.1
  72.2 0.6 copy.25
Async XLA Ops:
  68.4 3.1 %copy-start = (f32[256,256]{1,0:T(8,128)S(1)}, f32[256,256]{1,0:T(8,128)}, u32[]{:S(2)}) copy-start(f32[256,256]{1,0:T(8,128)} %get-tuple-element.26) | copy-start | bytes 786436
  68.4 3.8 %copy-start.1 = (f32[1,256]{1,0:T(1,128)S(1)}, f32[1,256]{1,0:T(1,128)}, u32[]{:S(2)}) copy-start(f32[1,256]{1,0:T(1,128)} %get-tuple-element.19) | copy-start | bytes 3076
where the time goes:
time: 72.9 us; the launch traced here: 72.7 us
  Pallas kernels  64.8 us (89%)
  local copies, waits for them, and re-layouts  6.66 us (9%)
  between operations  1.32 us (2%)
    pallas_call x1, Pallas kernels, exchange_return(): pl.pallas_call(functools.partial(return_kernel, n, scale), out_shape=(jax...  33.6 us
    pallas_call x1, Pallas kernels, exchange_gather(): pl.pallas_call(functools.partial(gather_kernel, n), out_shape=jax.ShapeDt...  15.9 us
    pallas_call x1, Pallas kernels, local_pass(): pl.pallas_call(local_kernel, out_shape=(jax.ShapeDtypeStruct(features.sha...  15.3 us
    unnamed x8, local copies, waits for them, and re-layouts  5.13 us

commit v1 on v0

--- a/solution.py
+++ b/solution.py
@@ -39,17 +39,20 @@
     )
 
 
-def live(count_ref, peer, values):
-    slot = lax.broadcasted_iota(jnp.int32, values.shape, 0)
-    return jnp.where(slot < count_ref[0, peer], values, jnp.zeros_like(values))
+def choose(n, count_ref, rows_ref, wide):
+    slots, lanes = rows_ref.shape[0], wide.shape[1]
+    slot = lax.broadcasted_iota(jnp.int32, (slots, 1), 0)
+    for p in range(n):
+        column = jnp.where(slot < count_ref[0, p], rows_ref[:, p : p + 1], -1)
+        wide[pl.ds(p * slots, slots), :] = jnp.broadcast_to(column, (slots, lanes))
 
 
 def gather_kernel(
-    n, count_ref, chosen_ref, features_hbm, halo_ref,
-    features_ref, total, sent, landed, send_sem, recv_sem, load_sem,
+    n, count_ref, rows_ref, features_hbm, halo_ref, chosen_ref,
+    features_ref, wide, total, sent, landed, send_sem, recv_sem, load_sem,
 ):
     me = lax.axis_index("dom")
-    slots = chosen_ref.shape[0]
+    slots = wide.shape[0]
     rows = features_ref.shape[0]
     step = math.gcd(rows, 512)
     loads = []
@@ -60,19 +63,24 @@
         )
         loads[c].start()
     barrier = greet(n, me)
+    choose(n, count_ref, rows_ref, wide)
+    lane = lax.broadcasted_iota(jnp.int32, wide.shape, 1)
+    lanes = wide.shape[1]
     for c in range(rows // step):
-        ids = lax.broadcasted_iota(jnp.int32, (slots, step), 1) + c * step
-        hot = jnp.where(ids == chosen_ref[...], 1.0, 0.0).astype(bf16)
+        hot = jnp.concatenate(
+            [
+                jnp.where(wide[...] == lane + (c * step + j), 1.0, 0.0).astype(bf16)
+                for j in range(0, step, lanes)
+            ],
+            axis=1,
+        )
         loads[c].wait()
         part = jnp.dot(hot, features_ref[pl.ds(c * step, step), :], preferred_element_type=f32)
         if c == 0:
             total[...] = part
         else:
             total[...] += part
-    slot_count = sent.shape[1]
-    for p in range(n):
-        block = total[pl.ds(p * slot_count, slot_count), :]
-        sent[p] = live(count_ref, p, block).astype(bf16)
+    sent[...] = total[...].astype(bf16).reshape(sent.shape)
     pl.semaphore_wait(barrier, n - 1)
     copy = functools.partial(push, n, me, lambda p: sent.at[p], landed, send_sem, recv_sem)
 
@@ -86,25 +94,35 @@
 
     lax.fori_loop(1, n, start, 0)
     landed[me] = sent[me]
+    chosen_ref[...] = wide[...].T[:1, :]
     lax.fori_loop(1, n, finish, 0)
     halo_ref[...] = landed[...]
 
 
-def exchange_gather(n, send_count, chosen, features, slot_count):
+LANES = 128
+
+
+def exchange_gather(n, send_count, send_rows, features):
     width = features.shape[1]
-    slots = chosen.shape[0]
+    slot_count = send_rows.shape[0]
+    slots = n * slot_count
     block = (n, slot_count, width)
+    vmem = pl.BlockSpec(memory_space=VMEM)
     return pl.pallas_call(
         functools.partial(gather_kernel, n),
-        out_shape=jax.ShapeDtypeStruct(block, bf16),
+        out_shape=(
+            jax.ShapeDtypeStruct(block, bf16),
+            jax.ShapeDtypeStruct((1, slots), jnp.int32),
+        ),
         in_specs=[
             pl.BlockSpec(memory_space=pltpu.SMEM),
-            pl.BlockSpec(memory_space=VMEM),
+            vmem,
             pl.BlockSpec(memory_space=pltpu.HBM),
         ],
-        out_specs=pl.BlockSpec(memory_space=VMEM),
+        out_specs=(vmem, vmem),
         scratch_shapes=[
             VMEM(features.shape, bf16),
+            VMEM((slots, LANES), jnp.int32),
             VMEM((slots, width), f32),
             VMEM(block, bf16),
             VMEM(block, bf16),
@@ -115,13 +133,8 @@
         compiler_params=pltpu.CompilerParams(
             collective_id=0, has_side_effects=True, vmem_limit_bytes=60 * 1024 * 1024
         ),
-        cost_estimate=pl.CostEstimate(
-            flops=2 * slots * features.shape[0] * width,
-            bytes_accessed=16 * features.size,
-            transcendentals=0,
-        ),
         name="gather_exchange",
-    )(send_count, chosen, features)
+    )(send_count, send_rows, features)
 
 
 GROUP = 8
@@ -288,22 +301,19 @@
 
 
 def return_kernel(
-    n, scale, count_ref, chosen_ref, halo_ref, weight_ref, bias_ref, own_hbm,
-    out_hbm, wsum_ref, bsum_ref,
-    halo_in, weight_in, bias_in, piece, pieces_in, returned, own, hot, out, load_sem, out_sem,
+    n, scale, halo_ref, weight_ref, bias_ref, halo_in, pieces_in, bsum_ref,
+    halo_land, weight_in, bias_in, piece, pieces_land,
     halo_s, halo_r, weight_s, weight_r, bias_s, bias_r, piece_s, piece_r,
 ):
     me = lax.axis_index("dom")
-    load = pltpu.make_async_copy(own_hbm, own, load_sem)
-    load.start()
     barrier = greet(n, me)
     pl.semaphore_wait(barrier, n - 1)
-    halo_copy = functools.partial(push, n, me, lambda p: halo_ref.at[p], halo_in, halo_s, halo_r)
+    halo_copy = functools.partial(push, n, me, lambda p: halo_ref.at[p], halo_land, halo_s, halo_r)
     weight_copy = functools.partial(
         push, n, me, lambda p: weight_ref.at[p], weight_in, weight_s, weight_r
     )
     bias_copy = functools.partial(push, n, me, lambda p: bias_ref, bias_in, bias_s, bias_r)
-    piece_copy = functools.partial(push, n, me, lambda p: piece, pieces_in, piece_s, piece_r)
+    piece_copy = functools.partial(push, n, me, lambda p: piece, pieces_land, piece_s, piece_r)
 
     def over(step):
         def turn(i, carry):
@@ -320,74 +330,95 @@
     over(lambda i: halo_copy(i).start())
     weight_in[me] = weight_ref[me]
     bias_in[me] = bias_ref[...]
-    halo_in[me] = halo_ref[me]
-    rows = own.shape[0]
-    slots = chosen_ref.shape[1]
-    step = math.gcd(rows, 512)
-    for c in range(rows // step):
-        ids = lax.broadcasted_iota(jnp.int32, (step, slots), 0) + c * step
-        hot[pl.ds(c * step, step), :] = jnp.where(ids == chosen_ref[...], 1.0, 0.0).astype(bf16)
+    halo_land[me] = halo_ref[me]
     over(lambda i: weight_copy(i).wait())
     piece[...] = (jnp.sum(weight_in[...].astype(f32), axis=0) * scale).astype(bf16)
     over(lambda i: piece_copy(i).start())
-    pieces_in[me] = piece[...]
+    pieces_land[me] = piece[...]
     over(lambda i: bias_copy(i).wait())
     bsum_ref[...] = jnp.sum(bias_in[...], axis=0) * scale
     over(lambda i: halo_copy(i).wait())
-    slot_count = halo_in.shape[1]
-    for p in range(n):
-        returned[pl.ds(p * slot_count, slot_count), :] = live(
-            count_ref, p, halo_in[p].astype(f32)
-        ).astype(bf16)
-    load.wait()
-    outs = []
-    for c in range(rows // step):
-        span = pl.ds(c * step, step)
-        collected = jnp.dot(hot[span, :], returned[...], preferred_element_type=f32)
-        out[span, :] = (own[span, :].astype(f32) + collected).astype(bf16)
-        outs.append(pltpu.make_async_copy(out.at[span], out_hbm.at[span], out_sem.at[c]))
-        outs[c].start()
+    halo_in[...] = halo_land[...]
     over(lambda i: piece_copy(i).wait())
-    piece_rows = piece.shape[0]
-    for p in range(n):
-        wsum_ref[pl.ds(p * piece_rows, piece_rows), :] = pieces_in[p].astype(f32)
-    for copy in outs:
-        copy.wait()
-
-
-def exchange_return(n, scale, send_count, chosen, halo_grad, weight_part, bias_part, own_grad):
-    rows, width = own_grad.shape
-    slots = chosen.shape[1]
+    pieces_in[...] = pieces_land[...]
+
+
+def exchange_return(n, scale, halo_grad, weight_part, bias_part):
     vmem = pl.BlockSpec(memory_space=VMEM)
-    hbm = pl.BlockSpec(memory_space=pltpu.HBM)
     return pl.pallas_call(
         functools.partial(return_kernel, n, scale),
         out_shape=(
-            jax.ShapeDtypeStruct(own_grad.shape, bf16),
-            jax.ShapeDtypeStruct((width, width), f32),
-            jax.ShapeDtypeStruct((1, width), f32),
-        ),
-        in_specs=[pl.BlockSpec(memory_space=pltpu.SMEM)] + [vmem] * 4 + [hbm],
-        out_specs=(hbm, vmem, vmem),
+            jax.ShapeDtypeStruct(halo_grad.shape, bf16),
+            jax.ShapeDtypeStruct(weight_part.shape, bf16),
+            jax.ShapeDtypeStruct(bias_part.shape, f32),
+        ),
+        in_specs=[vmem] * 3,
+        out_specs=(vmem,) * 3,
         scratch_shapes=[
             VMEM(halo_grad.shape, bf16),
             VMEM(weight_part.shape, bf16),
             VMEM((n,) + bias_part.shape, f32),
             VMEM(weight_part.shape[1:], bf16),
             VMEM(weight_part.shape, bf16),
-            VMEM((slots, width), bf16),
-            VMEM(own_grad.shape, bf16),
-            VMEM((rows, slots), bf16),
-            VMEM(own_grad.shape, bf16),
-            pltpu.SemaphoreType.DMA,
-            pltpu.SemaphoreType.DMA((rows // math.gcd(rows, 512),)),
         ]
         + [pltpu.SemaphoreType.DMA((n,))] * 8,
-        compiler_params=pltpu.CompilerParams(
-            collective_id=1, has_side_effects=True, vmem_limit_bytes=60 * 1024 * 1024
-        ),
+        compiler_params=pltpu.CompilerParams(collective_id=1, has_side_effects=True),
         name="return_exchange",
-    )(send_count, chosen, halo_grad, weight_part, bias_part, own_grad)
+    )(halo_grad, weight_part, bias_part)
+
+
+def final_kernel(
+    chosen_ref, returned, pieces, bias_sum, own_hbm, out_hbm, wsum_ref, bsum_ref,
+    own, out, load_sem, out_sem,
+):
+    rows = own.shape[0]
+    step = math.gcd(rows, 512)
+    spans = [pl.ds(c * step, step) for c in range(rows // step)]
+    loads = [
+        pltpu.make_async_copy(own_hbm.at[span], own.at[span], load_sem.at[c])
+        for c, span in enumerate(spans)
+    ]
+    for load in loads:
+        load.start()
+    wsum_ref[...] = pieces[...].astype(f32)
+    bsum_ref[...] = bias_sum[...]
+    slots = chosen_ref.shape[1]
+    ids = lax.broadcasted_iota(jnp.int32, (step, slots), 0)
+    outs = []
+    for c, span in enumerate(spans):
+        hot = jnp.where(ids == chosen_ref[...] - c * step, 1.0, 0.0).astype(bf16)
+        collected = jnp.dot(hot, returned[...], preferred_element_type=f32)
+        loads[c].wait()
+        out[span, :] = (own[span, :].astype(f32) + collected).astype(bf16)
+        outs.append(pltpu.make_async_copy(out.at[span], out_hbm.at[span], out_sem.at[c]))
+        outs[c].start()
+    for copy in outs:
+        copy.wait()
+
+
+def final_pass(chosen, returned, pieces, bias_sum, own_grad):
+    rows, width = own_grad.shape
+    vmem = pl.BlockSpec(memory_space=VMEM)
+    hbm = pl.BlockSpec(memory_space=pltpu.HBM)
+    steps = rows // math.gcd(rows, 512)
+    return pl.pallas_call(
+        final_kernel,
+        out_shape=(
+            jax.ShapeDtypeStruct(own_grad.shape, bf16),
+            jax.ShapeDtypeStruct(pieces.shape, f32),
+            jax.ShapeDtypeStruct(bias_sum.shape, f32),
+        ),
+        in_specs=[vmem] * 4 + [hbm],
+        out_specs=(hbm, vmem, vmem),
+        scratch_shapes=[
+            VMEM(own_grad.shape, bf16),
+            VMEM(own_grad.shape, bf16),
+            pltpu.SemaphoreType.DMA((steps,)),
+            pltpu.SemaphoreType.DMA((steps,)),
+        ],
+        compiler_params=pltpu.CompilerParams(vmem_limit_bytes=60 * 1024 * 1024),
+        name="final_pass",
+    )(chosen, returned, pieces, bias_sum, own_grad)
 
 
 def body(
@@ -398,18 +429,20 @@
     n = lax.axis_size("dom")
     slot_count = send_rows.shape[2]
     edge = tile_values.shape[1]
-    own = rows // edge
     slots = n * slot_count
-    halo = exchange_gather(n, send_count, send_rows.reshape(slots, 1), features, slot_count)
+    send_rows = jnp.swapaxes(send_rows, 1, 2).reshape(slot_count, n)
+    halo, chosen = exchange_gather(n, send_count, send_rows, features)
     blocks = lambda a: a.reshape(-1, edge, width)
     activation, own_grad, halo_grad, weight_part, bias_part = local_pass(
         n, tile_row, tile_col, tile_count, blocks(features), blocks(halo), tile_values,
         blocks(cotangent), weight, bias_vector.reshape(1, width),
     )
     scale = float(rows * n) ** (-0.5)
-    grad_features, weight_sum, bias_sum = exchange_return(
-        n, scale, send_count, send_rows.reshape(1, slots),
-        halo_grad.reshape(n, slot_count, width), weight_part, bias_part,
+    returned, pieces, bias_sum = exchange_return(
+        n, scale, halo_grad.reshape(n, slot_count, width), weight_part, bias_part
+    )
+    grad_features, weight_sum, bias_sum = final_pass(
+        chosen, returned.reshape(slots, width), pieces.reshape(width, width), bias_sum,
         own_grad.reshape(rows, width),
     )
     return (activation.reshape(rows, width), grad_features, weight_sum, bias_sum.reshape(width))

time: 72.9 us -> 73.4 us (level)
  Pallas kernels: 64.8 us -> 71.8 us
  local copies, waits for them, and re-layouts: 6.66 us -> 0 us
    pallas_call x1 -> x2, Pallas kernels: 15.9 us -> 23 us  [the longest x1 16.3 us: exchange_gather(): pl.pallas_call(functools.partial(gather_kernel, n), out_shape=(jax.ShapeD...]
    unnamed x8 -> x0, local copies, waits for them, and re-layouts: 5.13 us -> none
    reshape x2 -> x0, local copies, waits for them, and re-layouts: 1.53 us -> none  [the longest x1 0.86 us: body(): send_rows.reshape(slots, 1)]
    pallas_call x1, Pallas kernels: 33.6 us -> 32.3 us  [exchange_return(): pl.pallas_call(functools.partial(return_kernel, n, scale), out_shape=(jax...]
    pallas_call x1, Pallas kernels: 15.3 us -> 16.5 us  [local_pass(): pl.pallas_call(local_kernel, out_shape=(jax.ShapeDtypeStruct(features.sha...]
where the time goes in v1:
time: 73.4 us; the launch traced here: 73.1 us
  Pallas kernels  71.8 us (98%)
  between operations  1.3 us (2%)
    pallas_call x1, Pallas kernels, exchange_return(): pl.pallas_call(functools.partial(return_kernel, n, scale), out_shape=(jax...  32.3 us
    pallas_call x1, Pallas kernels, local_pass(): pl.pallas_call(local_kernel, out_shape=(jax.ShapeDtypeStruct(features.sha...  16.5 us
    pallas_call x1, Pallas kernels, exchange_gather(): pl.pallas_call(functools.partial(gather_kernel, n), out_shape=(jax.ShapeD...  16.3 us
    pallas_call x1, Pallas kernels, final_pass(): pl.pallas_call(final_kernel, out_shape=(jax.ShapeDtypeStruct(own_grad.sha...  6.68 us

profile of v1, /device:TPU:0, one launch (start us, length us, event | category | flops | bytes accessed | tf_op | source)
XLA Modules:
  0.0 73.1 jit_solution(14886670096892552929)
XLA Ops:
  1.3 16.3 %gather_exchange.1 = (bf16[32,16,256]{2,1,0:T(8,128)(2,1)}, s32[1,512]{1,0:T(1,128)}) custom-call(s32[1,32]{1,0:T(1,128)} %count_ref.1, s32[16,32]{1,0:T(8,128)} %bitcast.20, bf16[4096,256]{1,0:T(8,128)(2,1)} %features_hbm.1), custom_call_target="tpu_custom_call" | custom-call | tf_op jit(solution)/shard_map/gather_exchange/pallas_call | solution.py:111
  17.6 16.5 %local_pass.1 = (bf16[32,128,256]{2,1,0:T(8,128)(2,1)}, bf16[32,128,256]{2,1,0:T(8,128)(2,1)}, bf16[4,128,256]{2,1,0:T(8,128)(2,1)}, bf16[32,8,256]{2,1,0:T(8,128)(2,1)}, f32[1,256]{1,0:T(1,128)}) custom-call(s32[1,256]{1,0:T(1,128)} %tile_row.1, s32[1,256]{1,0:T(1,128)} %tile_col.1, s32[1]{0:T(128)S(6)} %copy.14.tile_count, bf16[32,128,256]{2,1,0:T(8,128)(2,1)} %bitcast.13, ...), custom_call_target="tpu_custom_call" | custom-call | tf_op jit(solution)/shard_map/local_pass/pallas_call | solution.py:270
  34.1 32.3 %return_exchange.1 = (bf16[32,16,256]{2,1,0:T(8,128)(2,1)}, bf16[32,8,256]{2,1,0:T(8,128)(2,1)}, f32[1,256]{1,0:T(1,128)}) custom-call(bf16[32,16,256]{2,1,0:T(8,128)(2,1)} %bitcast.17, bf16[32,8,256]{2,1,0:T(8,128)(2,1)} %get-tuple-element.21.weight_ref, f32[1,256]{1,0:T(1,128)} %get-tuple-element.22.bias_ref), custom_call_target="tpu_custom_call" | custom-call | tf_op jit(solution)/shard_map/return_exchange/pallas_call | solution.py:348
  66.4 6.7 %final_pass.1 = (bf16[4096,256]{1,0:T(8,128)(2,1)}, f32[256,256]{1,0:T(8,128)}, f32[1,256]{1,0:T(1,128)}) custom-call(s32[1,512]{1,0:T(1,128)} %get-tuple-element.19.chosen_ref, bf16[512,256]{1,0:T(8,128)(2,1)} %bitcast.18, bf16[256,256]{1,0:T(8,128)(2,1)} %bitcast.19, f32[1,256]{1,0:T(1,128)} %get-tuple-element.25.bias_sum, bf16[4096,256]{1,0:T(8,128)(2,1)} %bitcast.14), custom_call_target="tpu_custom_call" | custom-call | tf_op jit(solution)/shard_map/final_pass/pallas_call | solution.py:404

commit v2 on v1

v2 whole, which is shorter than its diff:
```python
import functools
import math

import jax
import jax.numpy as jnp
from jax import lax
from jax.experimental import pallas as pl
from jax.experimental.pallas import tpu as pltpu
from jax.sharding import PartitionSpec as P

MESH = pl.DeviceIdType.MESH
VMEM = pltpu.VMEM
f32 = jnp.float32
bf16 = jnp.bfloat16


def greet(n, me):
    barrier = pltpu.get_barrier_semaphore()

    def signal(i, carry):
        pl.semaphore_signal(
            barrier, inc=1, device_id=(lax.rem(me + i, n),), device_id_type=MESH
        )
        return carry

    lax.fori_loop(1, n, signal, 0)
    return barrier


def push(n, me, src, dst, send_sem, recv_sem, i):
    peer = lax.rem(me + i, n)
    return pltpu.make_async_remote_copy(
        src_ref=src(peer),
        dst_ref=dst.at[me],
        send_sem=send_sem.at[i],
        recv_sem=recv_sem.at[i],
        device_id=(peer,),
        device_id_type=MESH,
    )


LANES = 128
UNROLL = 8
CHUNK = 16
MIB = 1024 * 1024


def padded(size, step):
    return (size + step - 1) // step * step


def bits(size):
    return max(1, (size - 1).bit_length())


def pair_slots(number, keys):
    return padded((number + keys + 1) // 2, UNROLL)


def table_width(number, own):
    return padded(max(2 * pair_slots(number, own), number), LANES)


def down(row):
    return jnp.broadcast_to(row, (LANES, row.shape[1])).T


def iota(shape, dim):
    return lax.broadcasted_iota(jnp.int32, shape, dim)


def place(position, code, default, width):
    position, code = down(position), down(code - default)
    found = []
    for start in range(0, width, LANES):
        hit = position == iota(position.shape, 1) + start
        found.append(jnp.sum(jnp.where(hit, code, 0), axis=0, keepdims=True) + default)
    return jnp.concatenate(found, axis=1)


def wide_columns(columns, width):
    return jnp.concatenate([columns] * (width // LANES), axis=1)


def rank_of(same, valid):
    number = valid.shape[1]
    before = iota((number, number), 0) < iota((number, number), 1)
    taken = jnp.where(before & same, wide_columns(down(valid), number), 0)
    return jnp.sum(taken, axis=0, keepdims=True)


def pair_table(key, other, valid, zero, slots, width):
    number = key.shape[1]
    key_down, valid_down = down(key), down(valid)
    lane = iota((number, LANES), 1)
    count = jnp.sum(jnp.where(key_down == lane, valid_down, 0), axis=0, keepdims=True)
    pairs = (count + 1) // 2
    pairs_down = down(pairs)
    square = (LANES, LANES)
    upto = iota(square, 0) <= iota(square, 1)
    ends = jnp.sum(jnp.where(upto, pairs_down, 0), axis=0, keepdims=True)
    last = jnp.where(count > 0, ends - 1, slots)
    same = wide_columns(key_down, number) == key
    rank = rank_of(same, valid)
    lower = iota((LANES, number), 0) < key
    base = jnp.sum(jnp.where(lower, wide_columns(pairs_down, number), 0), axis=0, keepdims=True)
    position = jnp.where(valid > 0, 2 * base + rank, -1)
    tile = iota((1, number), 1)
    low, high = bits(number), bits(zero + 1)
    first = jnp.where(rank == 0, 1, 0)
    code = tile + other * (1 << low) + first * (1 << (low + high))
    return place(position, code, zero << low, width), last


def fill_table(table, row, col, count, own, ext):
    number = row.shape[1]
    width = table.shape[1]
    slots = pair_slots(number, own)
    used = iota((1, number), 1) < count
    mine = jnp.where(used & (col < own), 1, 0)
    far = jnp.where(used & (col >= own), 1, 0)
    table[...] = jnp.zeros_like(table)
    order, last = pair_table(row, col, mine, own, slots, width)
    table[0:1, :] = order
    table[1:2, :LANES] = last
    order, last = pair_table(col, row, mine, own, slots, width)
    table[2:3, :] = order
    table[3:4, :LANES] = last
    every = iota((number, number), 0) >= 0
    rank = rank_of(every, far)
    low, high = bits(number), bits(ext)
    code = iota((1, number), 1) + (col + row * (1 << high)) * (1 << low)
    position = jnp.where(far > 0, rank, -1)
    table[4:5, :] = place(position, code, (own + (own << high)) << low, width)
    total = jnp.sum(down(far), axis=0, keepdims=True)
    table[5:6, :LANES] = total


def choose(n, count_ref, rows_ref, wide):
    slots, lanes = rows_ref.shape[0], wide.shape[1]
    slot = iota((slots, 1), 0)
    for p in range(n):
        column = jnp.where(slot < count_ref[0, p], rows_ref[:, p : p + 1], -1)
        wide[pl.ds(p * slots, slots), :] = jnp.broadcast_to(column, (slots, lanes))


def run_pairs(table, line, number, zero, held, source, transposed, running, kept):
    low, high = bits(number), bits(zero + 1)
    slots = kept.shape[0] - 1
    kept[slots] = jnp.zeros(kept.shape[1:], kept.dtype)
    running[...] = jnp.zeros_like(running)
    axis = 0 if transposed else 1

    def turn(g, carry):
        total = running[...]
        for j in range(UNROLL):
            p = g * UNROLL + j
            one, two = table[line, 2 * p], table[line, 2 * p + 1]
            tiles = [held[code & ((1 << low) - 1)] for code in (one, two)]
            blocks = [source[(code >> low) & ((1 << high) - 1)] for code in (one, two)]
            product = lax.dot_general(
                jnp.concatenate(tiles, axis=axis), jnp.concatenate(blocks, axis=0),
                (((axis,), (0,)), ((), ())), preferred_element_type=f32,
            )
            keep = (1 - (one >> (low + high))).astype(f32)
            total = total * keep + product
            kept[p] = total.astype(kept.dtype)
        running[...] = total
        return carry

    lax.fori_loop(0, slots // UNROLL, turn, 0)


def gather_kernel(
    n, count_ref, tile_count, rows_ref, row_ref, col_ref, features_hbm, tiles_hbm,
    halo_ref, chosen_ref, table_ref, held, agg_ref,
    source, wide, total, sent, landed, table, running, kept,
    send_sem, recv_sem, load_sem, tile_sem, table_sem,
):
    me = lax.axis_index("dom")
    own = features_hbm.shape[0]
    edge, width = features_hbm.shape[1:]
    number = tiles_hbm.shape[0]
    step = math.gcd(own, 4)
    loads = []
    for c in range(own // step):
        span = pl.ds(c * step, step)
        loads.append(pltpu.make_async_copy(features_hbm.at[span], source.at[span], load_sem.at[c]))
        loads[c].start()
    chunk = math.gcd(number, CHUNK)
    tile_loads = []
    for c in range(number // chunk):
        span = pl.ds(c * chunk, chunk)
        tile_loads.append(pltpu.make_async_copy(tiles_hbm.at[span], held.at[span], tile_sem.at[c]))
        tile_loads[c].start()
    barrier = greet(n, me)
    choose(n, count_ref, rows_ref, wide)
    lane = iota(wide.shape, 1)
    for c in range(own // step):
        hot = jnp.concatenate(
            [
                jnp.where(wide[...] == lane + (c * step * edge + j), 1.0, 0.0).astype(bf16)
                for j in range(0, step * edge, LANES)
            ],
            axis=1,
        )
        loads[c].wait()
        block = source[pl.ds(c * step, step)].reshape(step * edge, width)
        part = jnp.dot(hot, block, preferred_element_type=f32)
        if c == 0:
            total[...] = part
        else:
            total[...] += part
    sent[...] = total[...].astype(bf16).reshape(sent.shape)
    pl.semaphore_wait(barrier, n - 1)
    copy = functools.partial(push, n, me, lambda p: sent.at[p], landed, send_sem, recv_sem)

    def start(i, carry):
        copy(i).start()
        return carry

    def finish(i, carry):
        copy(i).wait()
        return carry

    lax.fori_loop(1, n, start, 0)
    landed[me] = sent[me]
    ext = own + wide.shape[0] // edge
    fill_table(table_ref, row_ref[...], col_ref[...], tile_count[0], own, ext)
    move = pltpu.make_async_copy(table_ref, table, table_sem)
    move.start()
    chosen_ref[...] = wide[...].T[:1, :]
    source[own] = jnp.zeros((edge, width), bf16)
    for load in tile_loads:
        load.wait()
    move.wait()
    run_pairs(table, 0, number, own, held, source, False, running, kept)

    def pick(r, carry):
        agg_ref[r] = kept[table[1, r]]
        return carry

    lax.fori_loop(0, own, pick, 0)
    lax.fori_loop(1, n, finish, 0)
    halo_ref[...] = landed[...]


def exchange_gather(n, send_count, tile_count, send_rows, tile_row, tile_col, features, tiles):
    own, edge, width = features.shape
    number = tiles.shape[0]
    slot_count = send_rows.shape[0]
    slots = n * slot_count
    block = (n, slot_count, width)
    pairs = pair_slots(number, own)
    table = (8, table_width(number, own))
    vmem = pl.BlockSpec(memory_space=VMEM)
    smem = pl.BlockSpec(memory_space=pltpu.SMEM)
    hbm = pl.BlockSpec(memory_space=pltpu.HBM)
    dma = pltpu.SemaphoreType.DMA
    return pl.pallas_call(
        functools.partial(gather_kernel, n),
        out_shape=(
            jax.ShapeDtypeStruct(block, bf16),
            jax.ShapeDtypeStruct((1, slots), jnp.int32),
            jax.ShapeDtypeStruct(table, jnp.int32),
            jax.ShapeDtypeStruct(tiles.shape, bf16),
            jax.ShapeDtypeStruct(features.shape, bf16),
        ),
        in_specs=[smem, smem, vmem, vmem, vmem, hbm, hbm],
        out_specs=(vmem,) * 5,
        scratch_shapes=[
            VMEM((own + 1, edge, width), bf16),
            VMEM((slots, LANES), jnp.int32),
            VMEM((slots, width), f32),
            VMEM(block, bf16),
            VMEM(block, bf16),
            pltpu.SMEM(table, jnp.int32),
            VMEM((edge, width), f32),
            VMEM((pairs + 1, edge, width), bf16),
            dma((n,)),
            dma((n,)),
            dma((own // math.gcd(own, 4),)),
            dma((number // math.gcd(number, CHUNK),)),
            dma,
        ],
        compiler_params=pltpu.CompilerParams(
            collective_id=0, has_side_effects=True, vmem_limit_bytes=24 * MIB + slots * 8192
        ),
        name="gather_exchange",
    )(send_count, tile_count, send_rows, tile_row, tile_col, features, tiles)


GROUP = 4


def local_kernel(
    table, aggregate, halo, held, cotangent, weight, bias,
    activation, mixed, halo_grad, weight_part, bias_part,
    cot, act, extra, spread, wsum, bsum, cot_sem, act_sem,
):
    own = aggregate.shape[0]
    edge, width = aggregate.shape[1:]
    number = held.shape[0]
    far = halo.shape[0]
    low, high = bits(number), bits(own + far)
    step = math.gcd(own, 4)
    steps = own // step
    cot_copies = []
    for b in range(steps):
        span = pl.ds(b * step, step)
        cot_copies.append(pltpu.make_async_copy(cotangent.at[span], cot.at[span], cot_sem.at[b]))
        cot_copies[b].start()

    @pl.loop(0, own + 1)
    def _(r):
        extra[r] = jnp.zeros(extra.shape[1:], f32)

    spread[...] = jnp.zeros_like(spread)
    groups = (table[5, 0] + GROUP - 1) // GROUP

    def parts(s):
        code = table[4, s]
        return (
            code & ((1 << low) - 1), ((code >> low) & ((1 << high) - 1)) - own,
            code >> (low + high),
        )

    @pl.loop(0, groups)
    def _(g):
        for j in range(GROUP):
            k, col, row = parts(g * GROUP + j)
            extra[row] += jnp.dot(held[k], halo[col], preferred_element_type=f32)

    wsum[...] = jnp.zeros_like(wsum)
    bsum[...] = jnp.zeros_like(bsum)
    act_copies = []
    for b in range(steps):
        span = pl.ds(b * step, step)
        act_copies.append(pltpu.make_async_copy(act.at[span], activation.at[span], act_sem.at[b]))
        agg = (aggregate[span].astype(f32) + extra[span]).astype(bf16).reshape(step * edge, width)
        linear = jnp.dot(agg, weight[...], preferred_element_type=f32) + bias[...]
        sig = 0.5 * jnp.tanh(0.5 * linear) + 0.5
        value = linear * sig
        act[span] = value.astype(bf16).reshape(step, edge, width)
        act_copies[b].start()
        slope = sig + value * (1.0 - sig)
        cot_copies[b].wait()
        grad = (cot[span].reshape(step * edge, width).astype(f32) * slope).astype(bf16)
        wsum[...] += lax.dot_general(
            agg, grad, (((0,), (0,)), ((), ())), preferred_element_type=f32
        )
        bsum[...] += jnp.sum(grad.astype(f32), axis=0, keepdims=True)
        back = lax.dot_general(
            grad, weight[...], (((1,), (1,)), ((), ())), preferred_element_type=f32
        )
        mixed[span] = back.astype(bf16).reshape(step, edge, width)
    mixed[own] = jnp.zeros((edge, width), bf16)

    @pl.loop(0, groups)
    def _(g):
        for j in range(GROUP):
            s = g * GROUP + j
            k, col, row = parts(s)
            target = jnp.where(s < table[5, 0], col, far)
            spread[target] += lax.dot_general(
                held[k], mixed[row], (((0,), (0,)), ((), ())), preferred_element_type=f32
            )

    halo_grad[...] = spread[pl.ds(0, far)].astype(bf16)
    pieces, piece_rows = weight_part.shape[:2]
    for p in range(pieces):
        weight_part[p] = wsum[pl.ds(p * piece_rows, piece_rows), :].astype(bf16)
    bias_part[...] = bsum[...]
    for copy in act_copies:
        copy.wait()


def local_pass(n, table, aggregate, halo, held, cotangent, weight, bias):
    own, edge, width = aggregate.shape
    steps = own // math.gcd(own, 4)
    hbm = pl.BlockSpec(memory_space=pltpu.HBM)
    smem = pl.BlockSpec(memory_space=pltpu.SMEM)
    vmem = pl.BlockSpec(memory_space=VMEM)
    dma = pltpu.SemaphoreType.DMA
    return pl.pallas_call(
        local_kernel,
        out_shape=(
            jax.ShapeDtypeStruct(aggregate.shape, bf16),
            jax.ShapeDtypeStruct((own + 1, edge, width), bf16),
            jax.ShapeDtypeStruct(halo.shape, bf16),
            jax.ShapeDtypeStruct((n, width // n, width), bf16),
            jax.ShapeDtypeStruct((1, width), f32),
        ),
        in_specs=[smem, vmem, vmem, vmem, hbm, vmem, vmem],
        out_specs=(hbm, vmem, vmem, vmem, vmem),
        scratch_shapes=[
            VMEM(aggregate.shape, bf16),
            VMEM(aggregate.shape, bf16),
            VMEM((own + 1, edge, width), f32),
            VMEM((halo.shape[0] + 1, edge, width), f32),
            VMEM((width, width), f32),
            VMEM((1, width), f32),
            dma((steps,)),
            dma((steps,)),
        ],
        compiler_params=pltpu.CompilerParams(vmem_limit_bytes=24 * MIB + halo.size * 16),
        name="local_pass",
    )(table, aggregate, halo, held, cotangent, weight, bias)


def return_kernel(
    n, scale, table, held, mixed, halo_ref, weight_ref, bias_ref,
    halo_in, pieces_in, bsum_ref, own_grad,
    halo_land, weight_in, bias_in, piece, pieces_land, running, kept,
    halo_s, halo_r, weight_s, weight_r, bias_s, bias_r, piece_s, piece_r,
):
    me = lax.axis_index("dom")
    barrier = greet(n, me)
    halo_copy = functools.partial(push, n, me, lambda p: halo_ref.at[p], halo_land, halo_s, halo_r)
    weight_copy = functools.partial(
        push, n, me, lambda p: weight_ref.at[p], weight_in, weight_s, weight_r
    )
    bias_copy = functools.partial(push, n, me, lambda p: bias_ref, bias_in, bias_s, bias_r)
    piece_copy = functools.partial(push, n, me, lambda p: piece, pieces_land, piece_s, piece_r)

    def over(step):
        def turn(i, carry):
            step(i)
            return carry

        lax.fori_loop(1, n, turn, 0)

    def first(i):
        weight_copy(i).start()
        bias_copy(i).start()

    pl.semaphore_wait(barrier, n - 1)
    over(first)
    over(lambda i: halo_copy(i).start())
    weight_in[me] = weight_ref[me]
    bias_in[me] = bias_ref[...]
    halo_land[me] = halo_ref[me]
    number = held.shape[0]
    own = mixed.shape[0] - 1
    run_pairs(table, 2, number, own, held, mixed, True, running, kept)
    over(lambda i: weight_copy(i).wait())
    piece[...] = (jnp.sum(weight_in[...].astype(f32), axis=0) * scale).astype(bf16)
    over(lambda i: piece_copy(i).start())
    pieces_land[me] = piece[...]

    def pick(c, carry):
        own_grad[c] = kept[table[3, c]]
        return carry

    lax.fori_loop(0, own, pick, 0)
    over(lambda i: bias_copy(i).wait())
    bsum_ref[...] = jnp.sum(bias_in[...], axis=0) * scale
    over(lambda i: halo_copy(i).wait())
    halo_in[...] = halo_land[...]
    over(lambda i: piece_copy(i).wait())
    pieces_in[...] = pieces_land[...]


def exchange_return(n, scale, table, held, mixed, halo_grad, weight_part, bias_part):
    vmem = pl.BlockSpec(memory_space=VMEM)
    smem = pl.BlockSpec(memory_space=pltpu.SMEM)
    edge, width = mixed.shape[1:]
    own = mixed.shape[0] - 1
    pairs = pair_slots(held.shape[0], own)
    return pl.pallas_call(
        functools.partial(return_kernel, n, scale),
        out_shape=(
            jax.ShapeDtypeStruct(halo_grad.shape, bf16),
            jax.ShapeDtypeStruct(weight_part.shape, bf16),
            jax.ShapeDtypeStruct(bias_part.shape, f32),
            jax.ShapeDtypeStruct((own, edge, width), bf16),
        ),
        in_specs=[smem] + [vmem] * 5,
        out_specs=(vmem,) * 4,
        scratch_shapes=[
            VMEM(halo_grad.shape, bf16),
            VMEM(weight_part.shape, bf16),
            VMEM((n,) + bias_part.shape, f32),
            VMEM(weight_part.shape[1:], bf16),
            VMEM(weight_part.shape, bf16),
            VMEM((edge, width), f32),
            VMEM((pairs + 1, edge, width), bf16),
        ]
        + [pltpu.SemaphoreType.DMA((n,))] * 8,
        compiler_params=pltpu.CompilerParams(
            collective_id=1, has_side_effects=True,
            vmem_limit_bytes=20 * MIB + halo_grad.size * 16,
        ),
        name="return_exchange",
    )(table, held, mixed, halo_grad, weight_part, bias_part)


def final_kernel(
    chosen_ref, returned, pieces, bias_sum, own, out_hbm, wsum_hbm, bsum_hbm,
    out, wsum, bsum, out_sem, small_sem,
):
    rows = own.shape[0]
    step = math.gcd(rows, 512)
    spans = [pl.ds(c * step, step) for c in range(rows // step)]
    wsum[...] = pieces[...].astype(f32)
    bsum[...] = bias_sum[...]
    outs = [
        pltpu.make_async_copy(wsum, wsum_hbm, small_sem.at[0]),
        pltpu.make_async_copy(bsum, bsum_hbm, small_sem.at[1]),
    ]
    for copy in outs:
        copy.start()
    slots = chosen_ref.shape[1]
    ids = iota((step, slots), 0)
    for c, span in enumerate(spans):
        hot = jnp.where(ids == chosen_ref[...] - c * step, 1.0, 0.0).astype(bf16)
        collected = jnp.dot(hot, returned[...], preferred_element_type=f32)
        out[span, :] = (own[span, :].astype(f32) + collected).astype(bf16)
        copy = pltpu.make_async_copy(out.at[span], out_hbm.at[span], out_sem.at[c])
        copy.start()
        outs.append(copy)
    for copy in outs:
        copy.wait()


def final_pass(chosen, returned, pieces, bias_sum, own_grad):
    rows, width = own_grad.shape
    vmem = pl.BlockSpec(memory_space=VMEM)
    hbm = pl.BlockSpec(memory_space=pltpu.HBM)
    steps = rows // math.gcd(rows, 512)
    return pl.pallas_call(
        final_kernel,
        out_shape=(
            jax.ShapeDtypeStruct(own_grad.shape, bf16),
            jax.ShapeDtypeStruct(pieces.shape, f32),
            jax.ShapeDtypeStruct(bias_sum.shape, f32),
        ),
        in_specs=[vmem] * 5,
        out_specs=(hbm,) * 3,
        scratch_shapes=[
            VMEM(own_grad.shape, bf16),
            VMEM(pieces.shape, f32),
            VMEM(bias_sum.shape, f32),
            pltpu.SemaphoreType.DMA((steps,)),
            pltpu.SemaphoreType.DMA((2,)),
        ],
        compiler_params=pltpu.CompilerParams(vmem_limit_bytes=12 * MIB + returned.size * 32),
        name="final_pass",
    )(chosen, returned, pieces, bias_sum, own_grad)


def body(
    features, weight, bias_vector, tile_values, tile_row, tile_col, tile_count, send_rows,
    send_count, cotangent,
):
    rows, width = features.shape
    n = lax.axis_size("dom")
    slot_count = send_rows.shape[2]
    edge = tile_values.shape[1]
    slots = n * slot_count
    send_rows = jnp.swapaxes(send_rows, 1, 2).reshape(slot_count, n)
    blocks = lambda a: a.reshape(-1, edge, width)
    halo, chosen, table, held, aggregate = exchange_gather(
        n, send_count, tile_count, send_rows, tile_row, tile_col, blocks(features), tile_values
    )
    activation, mixed, halo_grad, weight_part, bias_part = local_pass(
        n, table, aggregate, blocks(halo), held, blocks(cotangent), weight,
        bias_vector.reshape(1, width),
    )
    scale = float(rows * n) ** (-0.5)
    returned, pieces, bias_sum, own_grad = exchange_return(
        n, scale, table, held, mixed, halo_grad.reshape(n, slot_count, width), weight_part,
        bias_part,
    )
    grad_features, weight_sum, bias_sum = final_pass(
        chosen, returned.reshape(slots, width), pieces.reshape(width, width), bias_sum,
        own_grad.reshape(rows, width),
    )
    return (activation.reshape(rows, width), grad_features, weight_sum, bias_sum.reshape(width))


def solution(mesh):
    return jax.shard_map(
        body,
        mesh=mesh,
        in_specs=(
            P("dom", None),
            P(),
            P(),
            P("dom", None, None),
            P("dom", None),
            P("dom", None),
            P("dom"),
            P("dom", None, None),
            P("dom", None),
            P("dom", None),
        ),
        out_specs=(P("dom", None), P("dom", None), P(), P()),
        check_vma=False,
    )
```

time: 73.4 us -> 57.7 us (0.79); the launches traced: 73.1 us -> 58.2 us
  Pallas kernels: 71.8 us -> 49.2 us
  local copies, waits for them, and re-layouts: 0 us -> 7.68 us
    pallas_call x1, Pallas kernels: 32.3 us -> 22.6 us  [exchange_return(): pl.pallas_call(functools.partial(return_kernel, n, scale), out_shape=(jax...]
    pallas_call x1, Pallas kernels: 16.5 us -> 7.12 us  [local_pass(): pl.pallas_call(local_kernel, out_shape=(jax.ShapeDtypeStruct(aggregate.sh...]
    unnamed x0 -> x18, local copies, waits for them, and re-layouts: none -> 7.68 us
    pallas_call x1, Pallas kernels: 6.68 us -> 2.31 us  [final_pass(): pl.pallas_call(final_kernel, out_shape=(jax.ShapeDtypeStruct(own_grad.sha...]
    pallas_call x1, Pallas kernels: 16.3 us -> 17.1 us  [exchange_gather(): pl.pallas_call(functools.partial(gather_kernel, n), out_shape=(jax.ShapeD...]
where the time goes in v2:
time: 57.7 us; the launch traced here: 58.2 us
  Pallas kernels  49.2 us (85%)
  local copies, waits for them, and re-layouts  7.68 us (13%)
  between operations  1.34 us (2%)
    pallas_call x1, Pallas kernels, exchange_return(): pl.pallas_call(functools.partial(return_kernel, n, scale), out_shape=(jax...  22.6 us
    pallas_call x1, Pallas kernels, exchange_gather(): pl.pallas_call(functools.partial(gather_kernel, n), out_shape=(jax.ShapeD...  17.1 us
    unnamed x18, local copies, waits for them, and re-layouts  7.68 us
    pallas_call x1, Pallas kernels, local_pass(): pl.pallas_call(local_kernel, out_shape=(jax.ShapeDtypeStruct(aggregate.sh...  7.12 us
    pallas_call x1, Pallas kernels, final_pass(): pl.pallas_call(final_kernel, out_shape=(jax.ShapeDtypeStruct(own_grad.sha...  2.31 us

profile of v2, /device:TPU:0, one launch (start us, length us, event | category | flops | bytes accessed | tf_op | source)
XLA Modules:
  0.0 58.2 jit_solution(803212087450199135)
XLA Ops:
  1.3 0.0 copy-start
  1.3 3.4 %copy-done = bf16[256,128,128]{2,1,0:T(8,128)(2,1)S(1)} copy-done((bf16[256,128,128]{2,1,0:T(8,128)(2,1)S(1)}, bf16[256,128,128]{2,1,0:T(8,128)(2,1)}, u32[]{:S(2)}) %copy-start) | copy-done | bytes 8388632
  4.7 0.0 copy-start.1
  4.7 1.6 %copy-done.1 = bf16[4096,256]{1,0:T(8,128)(2,1)S(1)} copy-done((bf16[4096,256]{1,0:T(8,128)(2,1)S(1)}, bf16[4096,256]{1,0:T(8,128)(2,1)}, u32[]{:S(2)}) %copy-start.1) | copy-done | bytes 2097176
  6.3 0.0 copy-start.4
  6.3 0.7 %copy-done.4 = s32[1,32,16]{1,2,0:T(8,128)S(1)} copy-done((s32[1,32,16]{1,2,0:T(8,128)S(1)}, s32[1,32,16]{1,2,0:T(8,128)}, u32[]{:S(2)}) %copy-start.4) | copy-done | bytes 2072
  7.0 0.0 copy-start.6
  7.0 0.7 %copy-done.6 = s32[1,256]{1,0:T(1,128)S(1)} copy-done((s32[1,256]{1,0:T(1,128)S(1)}, s32[1,256]{1,0:T(1,128)}, u32[]{:S(2)}) %copy-start.6) | copy-done | bytes 1048
  7.6 0.0 copy-start.7
  7.6 0.7 %copy-done.7 = s32[1,256]{1,0:T(1,128)S(1)} copy-done((s32[1,256]{1,0:T(1,128)S(1)}, s32[1,256]{1,0:T(1,128)}, u32[]{:S(2)}) %copy-start.7) | copy-done | bytes 1048
  8.3 0.0 copy-start.8
  8.3 0.7 %copy-done.8 = s32[1,32]{1,0:T(1,128)S(1)} copy-done((s32[1,32]{1,0:T(1,128)S(1)}, s32[1,32]{1,0:T(1,128)}, u32[]{:S(2)}) %copy-start.8) | copy-done | bytes 152
  9.0 0.0 copy-start.2
  9.0 0.0 copy-start.3
  9.0 0.0 copy-start.5
  9.0 17.1 %gather_exchange.1 = (bf16[32,16,256]{2,1,0:T(8,128)(2,1)S(1)}, s32[1,512]{1,0:T(1,128)S(1)}, s32[8,384]{1,0:T(8,128)S(1)}, bf16[256,128,128]{2,1,0:T(8,128)(2,1)S(1)}, bf16[32,128,256]{2,1,0:T(8,128)(2,1)S(1)}) custom-call(s32[1,32]{1,0:T(1,128)S(1)} %copy-done.8, s32[1]{0:T(128)S(6)} %copy.14.tile_count, s32[16,32]{1,0:T(8,128)S(1)} %bitcast.20, ...), custom_call_target="tpu_custom_call" | custom-call | tf_op jit(solution)/shard_map/gather_exchange/pallas_call | solution.py:260
  26.1 0.0 copy-done.2
  26.1 0.0 copy-done.3
  26.1 0.0 copy-done.5
  26.1 7.1 %local_pass.1 = (bf16[32,128,256]{2,1,0:T(8,128)(2,1)}, bf16[33,128,256]{2,1,0:T(8,128)(2,1)S(1)}, bf16[4,128,256]{2,1,0:T(8,128)(2,1)S(1)}, bf16[32,8,256]{2,1,0:T(8,128)(2,1)S(1)}, f32[1,256]{1,0:T(1,128)S(1)}) custom-call(s32[8,384]{1,0:T(8,128)S(1)} %get-tuple-element.21.table, bf16[32,128,256]{2,1,0:T(8,128)(2,1)S(1)} %get-tuple-element.22.aggregate, ...), custom_call_target="tpu_custom_call" | custom-call | tf_op jit(solution)/shard_map/local_pass/pallas_call | solution.py:385
  33.3 22.6 %return_exchange.1 = (bf16[32,16,256]{2,1,0:T(8,128)(2,1)S(1)}, bf16[32,8,256]{2,1,0:T(8,128)(2,1)S(1)}, f32[1,256]{1,0:T(1,128)S(1)}, bf16[32,128,256]{2,1,0:T(8,128)(2,1)S(1)}) custom-call(s32[8,384]{1,0:T(8,128)S(1)} %get-tuple-element.21.table, bf16[256,128,128]{2,1,0:T(8,128)(2,1)S(1)} %get-tuple-element.24.held, ...), custom_call_target="tpu_custom_call" | custom-call | tf_op jit(solution)/shard_map/return_exchange/pallas_call | solution.py:470
  55.9 2.3 %final_pass.1 = (bf16[4096,256]{1,0:T(8,128)(2,1)}, f32[256,256]{1,0:T(8,128)}, f32[1,256]{1,0:T(1,128)}) custom-call(s32[1,512]{1,0:T(1,128)S(1)} %get-tuple-element.26.chosen_ref, bf16[512,256]{1,0:T(8,128)(2,1)S(1)} %bitcast.18, bf16[256,256]{1,0:T(8,128)(2,1)S(1)} %bitcast.19, f32[1,256]{1,0:T(1,128)S(1)} %get-tuple-element.33.bias_sum, ...), custom_call_target="tpu_custom_call" | custom-call | tf_op jit(solution)/shard_map/final_pass/pallas_call | solution.py:531
Async XLA Ops:
  1.3 3.4 %copy-start = (bf16[256,128,128]{2,1,0:T(8,128)(2,1)S(1)}, bf16[256,128,128]{2,1,0:T(8,128)(2,1)}, u32[]{:S(2)}) copy-start(bf16[256,128,128]{2,1,0:T(8,128)(2,1)} %tiles_hbm.1) | copy-start | bytes 25165828
  4.7 1.6 %copy-start.1 = (bf16[4096,256]{1,0:T(8,128)(2,1)S(1)}, bf16[4096,256]{1,0:T(8,128)(2,1)}, u32[]{:S(2)}) copy-start(bf16[4096,256]{1,0:T(8,128)(2,1)} %param.10) | copy-start | bytes 6291460
  6.3 0.7 %copy-start.4 = (s32[1,32,16]{1,2,0:T(8,128)S(1)}, s32[1,32,16]{1,2,0:T(8,128)}, u32[]{:S(2)}) copy-start(s32[1,32,16]{1,2,0:T(8,128)} %param.17) | copy-start | bytes 6148
  7.0 0.7 %copy-start.6 = (s32[1,256]{1,0:T(1,128)S(1)}, s32[1,256]{1,0:T(1,128)}, u32[]{:S(2)}) copy-start(s32[1,256]{1,0:T(1,128)} %row_ref.1) | copy-start | bytes 3076
  7.6 0.7 %copy-start.7 = (s32[1,256]{1,0:T(1,128)S(1)}, s32[1,256]{1,0:T(1,128)}, u32[]{:S(2)}) copy-start(s32[1,256]{1,0:T(1,128)} %col_ref.1) | copy-start | bytes 3076
  8.3 0.7 %copy-start.8 = (s32[1,32]{1,0:T(1,128)S(1)}, s32[1,32]{1,0:T(1,128)}, u32[]{:S(2)}) copy-start(s32[1,32]{1,0:T(1,128)} %count_ref.1) | copy-start | bytes 388
  9.0 17.1 %copy-start.2 = (bf16[4096,256]{1,0:T(8,128)(2,1)S(1)}, bf16[4096,256]{1,0:T(8,128)(2,1)}, u32[]{:S(2)}) copy-start(bf16[4096,256]{1,0:T(8,128)(2,1)} %param.19) | copy-start | bytes 6291460
  9.0 17.2 %copy-start.3 = (bf16[256,256]{1,0:T(8,128)(2,1)S(1)}, bf16[256,256]{1,0:T(8,128)(2,1)}, u32[]{:S(2)}) copy-start(bf16[256,256]{1,0:T(8,128)(2,1)} %weight.1) | copy-start | bytes 393220
  9.0 17.2 %copy-start.5 = (f32[256]{0:T(256)S(1)}, f32[256]{0:T(256)}, u32[]{:S(2)}) copy-start(f32[256]{0:T(256)} %param.12) | copy-start | bytes 3076

commit v3 on v2

--- a/solution.py
+++ b/solution.py
@@ -41,6 +41,7 @@
 
 LANES = 128
 UNROLL = 8
+NEAR = 8
 CHUNK = 16
 MIB = 1024 * 1024
 
@@ -144,11 +145,12 @@
         wide[pl.ds(p * slots, slots), :] = jnp.broadcast_to(column, (slots, lanes))
 
 
-def run_pairs(table, line, number, zero, held, source, transposed, running, kept):
+def run_pairs(table, line, number, zero, held, source, transposed, running, kept, begin, end):
     low, high = bits(number), bits(zero + 1)
     slots = kept.shape[0] - 1
-    kept[slots] = jnp.zeros(kept.shape[1:], kept.dtype)
-    running[...] = jnp.zeros_like(running)
+    if begin == 0:
+        kept[slots] = jnp.zeros(kept.shape[1:], kept.dtype)
+        running[...] = jnp.zeros_like(running)
     axis = 0 if transposed else 1
 
     def turn(g, carry):
@@ -168,20 +170,29 @@
         running[...] = total
         return carry
 
-    lax.fori_loop(0, slots // UNROLL, turn, 0)
+    lax.fori_loop(begin, end, turn, 0)
 
 
 def gather_kernel(
-    n, count_ref, tile_count, rows_ref, row_ref, col_ref, features_hbm, tiles_hbm,
+    n, tile_count, count_hbm, rows_hbm, row_hbm, col_hbm, features_hbm, tiles_hbm,
     halo_ref, chosen_ref, table_ref, held, agg_ref,
+    count_ref, rows_ref, row_ref, col_ref,
     source, wide, total, sent, landed, table, running, kept,
-    send_sem, recv_sem, load_sem, tile_sem, table_sem,
+    send_sem, recv_sem, load_sem, tile_sem, table_sem, small_sem,
 ):
     me = lax.axis_index("dom")
     own = features_hbm.shape[0]
     edge, width = features_hbm.shape[1:]
     number = tiles_hbm.shape[0]
     step = math.gcd(own, 4)
+    smalls = [
+        pltpu.make_async_copy(count_hbm, count_ref, small_sem.at[0]),
+        pltpu.make_async_copy(rows_hbm, rows_ref, small_sem.at[1]),
+        pltpu.make_async_copy(row_hbm, row_ref, small_sem.at[2]),
+        pltpu.make_async_copy(col_hbm, col_ref, small_sem.at[3]),
+    ]
+    for copy in smalls:
+        copy.start()
     loads = []
     for c in range(own // step):
         span = pl.ds(c * step, step)
@@ -194,6 +205,8 @@
         tile_loads.append(pltpu.make_async_copy(tiles_hbm.at[span], held.at[span], tile_sem.at[c]))
         tile_loads[c].start()
     barrier = greet(n, me)
+    for copy in smalls:
+        copy.wait()
     choose(n, count_ref, rows_ref, wide)
     lane = iota(wide.shape, 1)
     for c in range(own // step):
@@ -234,7 +247,8 @@
     for load in tile_loads:
         load.wait()
     move.wait()
-    run_pairs(table, 0, number, own, held, source, False, running, kept)
+    turns = (kept.shape[0] - 1) // UNROLL
+    run_pairs(table, 0, number, own, held, source, False, running, kept, 0, turns)
 
     def pick(r, carry):
         agg_ref[r] = kept[table[1, r]]
@@ -266,9 +280,13 @@
             jax.ShapeDtypeStruct(tiles.shape, bf16),
             jax.ShapeDtypeStruct(features.shape, bf16),
         ),
-        in_specs=[smem, smem, vmem, vmem, vmem, hbm, hbm],
+        in_specs=[smem] + [hbm] * 6,
         out_specs=(vmem,) * 5,
         scratch_shapes=[
+            pltpu.SMEM(send_count.shape, jnp.int32),
+            VMEM(send_rows.shape, jnp.int32),
+            VMEM(tile_row.shape, jnp.int32),
+            VMEM(tile_col.shape, jnp.int32),
             VMEM((own + 1, edge, width), bf16),
             VMEM((slots, LANES), jnp.int32),
             VMEM((slots, width), f32),
@@ -282,12 +300,19 @@
             dma((own // math.gcd(own, 4),)),
             dma((number // math.gcd(number, CHUNK),)),
             dma,
+            dma((4,)),
         ],
         compiler_params=pltpu.CompilerParams(
             collective_id=0, has_side_effects=True, vmem_limit_bytes=24 * MIB + slots * 8192
         ),
         name="gather_exchange",
-    )(send_count, tile_count, send_rows, tile_row, tile_col, features, tiles)
+    )(
+        tile_count,
+        *[
+            pltpu.with_memory_space_constraint(a, pltpu.HBM)
+            for a in (send_count, send_rows, tile_row, tile_col, features, tiles)
+        ],
+    )
 
 
 GROUP = 4
@@ -375,7 +400,7 @@
         copy.wait()
 
 
-def local_pass(n, table, aggregate, halo, held, cotangent, weight, bias):
+def local_pass(near, table, aggregate, halo, held, cotangent, weight, bias):
     own, edge, width = aggregate.shape
     steps = own // math.gcd(own, 4)
     hbm = pl.BlockSpec(memory_space=pltpu.HBM)
@@ -388,7 +413,7 @@
             jax.ShapeDtypeStruct(aggregate.shape, bf16),
             jax.ShapeDtypeStruct((own + 1, edge, width), bf16),
             jax.ShapeDtypeStruct(halo.shape, bf16),
-            jax.ShapeDtypeStruct((n, width // n, width), bf16),
+            jax.ShapeDtypeStruct((near, width // near, width), bf16),
             jax.ShapeDtypeStruct((1, width), f32),
         ),
         in_specs=[smem, vmem, vmem, vmem, hbm, vmem, vmem],
@@ -411,62 +436,86 @@
 def return_kernel(
     n, scale, table, held, mixed, halo_ref, weight_ref, bias_ref,
     halo_in, pieces_in, bsum_ref, own_grad,
-    halo_land, weight_in, bias_in, piece, pieces_land, running, kept,
-    halo_s, halo_r, weight_s, weight_r, bias_s, bias_r, piece_s, piece_r,
+    halo_land, bias_in, near_in, mine, far_in, piece, pieces_land, running, kept,
+    halo_s, halo_r, bias_s, bias_r, near_s, near_r, far_s, far_r, piece_s, piece_r,
 ):
     me = lax.axis_index("dom")
     barrier = greet(n, me)
+    near = weight_ref.shape[0]
+    far = n // near
+    block, seat = lax.div(me, near), lax.rem(me, near)
+    number = held.shape[0]
+    own = mixed.shape[0] - 1
+    turns = (kept.shape[0] - 1) // UNROLL
+    early = turns // 3
+    pairs = functools.partial(run_pairs, table, 2, number, own, held, mixed, True, running, kept)
+    pairs(0, early)
     halo_copy = functools.partial(push, n, me, lambda p: halo_ref.at[p], halo_land, halo_s, halo_r)
-    weight_copy = functools.partial(
-        push, n, me, lambda p: weight_ref.at[p], weight_in, weight_s, weight_r
-    )
     bias_copy = functools.partial(push, n, me, lambda p: bias_ref, bias_in, bias_s, bias_r)
-    piece_copy = functools.partial(push, n, me, lambda p: piece, pieces_land, piece_s, piece_r)
-
-    def over(step):
+
+    def inside(src, dst, send_sem, recv_sem, i):
+        peer = lax.rem(seat + i, near)
+        return pltpu.make_async_remote_copy(
+            src_ref=src(peer), dst_ref=dst.at[seat], send_sem=send_sem.at[i],
+            recv_sem=recv_sem.at[i], device_id=(block * near + peer,), device_id_type=MESH,
+        )
+
+    def across(i):
+        peer = lax.rem(block + i, far)
+        return pltpu.make_async_remote_copy(
+            src_ref=mine, dst_ref=far_in.at[block], send_sem=far_s.at[i],
+            recv_sem=far_r.at[i], device_id=(peer * near + seat,), device_id_type=MESH,
+        )
+
+    near_copy = functools.partial(inside, lambda p: weight_ref.at[p], near_in, near_s, near_r)
+    piece_copy = functools.partial(inside, lambda p: piece, pieces_land, piece_s, piece_r)
+
+    def over(count, step):
         def turn(i, carry):
             step(i)
             return carry
 
-        lax.fori_loop(1, n, turn, 0)
-
-    def first(i):
-        weight_copy(i).start()
-        bias_copy(i).start()
+        lax.fori_loop(1, count, turn, 0)
 
     pl.semaphore_wait(barrier, n - 1)
-    over(first)
-    over(lambda i: halo_copy(i).start())
-    weight_in[me] = weight_ref[me]
+    over(near, lambda i: near_copy(i).start())
+    over(n, lambda i: halo_copy(i).start())
+    over(n, lambda i: bias_copy(i).start())
+    near_in[seat] = weight_ref[seat]
     bias_in[me] = bias_ref[...]
     halo_land[me] = halo_ref[me]
-    number = held.shape[0]
-    own = mixed.shape[0] - 1
-    run_pairs(table, 2, number, own, held, mixed, True, running, kept)
-    over(lambda i: weight_copy(i).wait())
-    piece[...] = (jnp.sum(weight_in[...].astype(f32), axis=0) * scale).astype(bf16)
-    over(lambda i: piece_copy(i).start())
-    pieces_land[me] = piece[...]
+    pairs(early, turns)
+    over(near, lambda i: near_copy(i).wait())
+    mine[...] = jnp.sum(near_in[...].astype(f32), axis=0).astype(bf16)
+    over(far, lambda i: across(i).start())
+    far_in[block] = mine[...]
 
     def pick(c, carry):
         own_grad[c] = kept[table[3, c]]
         return carry
 
     lax.fori_loop(0, own, pick, 0)
-    over(lambda i: bias_copy(i).wait())
+    over(far, lambda i: across(i).wait())
+    piece[...] = (jnp.sum(far_in[...].astype(f32), axis=0) * scale).astype(bf16)
+    over(near, lambda i: piece_copy(i).start())
+    pieces_land[seat] = piece[...]
+    over(n, lambda i: bias_copy(i).wait())
     bsum_ref[...] = jnp.sum(bias_in[...], axis=0) * scale
-    over(lambda i: halo_copy(i).wait())
+    over(n, lambda i: halo_copy(i).wait())
     halo_in[...] = halo_land[...]
-    over(lambda i: piece_copy(i).wait())
+    over(near, lambda i: piece_copy(i).wait())
     pieces_in[...] = pieces_land[...]
 
 
 def exchange_return(n, scale, table, held, mixed, halo_grad, weight_part, bias_part):
     vmem = pl.BlockSpec(memory_space=VMEM)
     smem = pl.BlockSpec(memory_space=pltpu.SMEM)
+    dma = pltpu.SemaphoreType.DMA
     edge, width = mixed.shape[1:]
     own = mixed.shape[0] - 1
     pairs = pair_slots(held.shape[0], own)
+    near = weight_part.shape[0]
+    piece = weight_part.shape[1:]
     return pl.pallas_call(
         functools.partial(return_kernel, n, scale),
         out_shape=(
@@ -479,14 +528,19 @@
         out_specs=(vmem,) * 4,
         scratch_shapes=[
             VMEM(halo_grad.shape, bf16),
+            VMEM((n,) + bias_part.shape, f32),
             VMEM(weight_part.shape, bf16),
-            VMEM((n,) + bias_part.shape, f32),
-            VMEM(weight_part.shape[1:], bf16),
+            VMEM(piece, bf16),
+            VMEM((n // near,) + piece, bf16),
+            VMEM(piece, bf16),
             VMEM(weight_part.shape, bf16),
             VMEM((edge, width), f32),
             VMEM((pairs + 1, edge, width), bf16),
         ]
-        + [pltpu.SemaphoreType.DMA((n,))] * 8,
+        + [dma((n,))] * 4
+        + [dma((near,))] * 2
+        + [dma((n // near,))] * 2
+        + [dma((near,))] * 2,
         compiler_params=pltpu.CompilerParams(
             collective_id=1, has_side_effects=True,
             vmem_limit_bytes=20 * MIB + halo_grad.size * 16,
@@ -564,7 +618,7 @@
         n, send_count, tile_count, send_rows, tile_row, tile_col, blocks(features), tile_values
     )
     activation, mixed, halo_grad, weight_part, bias_part = local_pass(
-        n, table, aggregate, blocks(halo), held, blocks(cotangent), weight,
+        math.gcd(n, NEAR), table, aggregate, blocks(halo), held, blocks(cotangent), weight,
         bias_vector.reshape(1, width),
     )
     scale = float(rows * n) ** (-0.5)

time: 57.7 us -> 50.4 us (0.87)
  local copies, waits for them, and re-layouts: 7.68 us -> 0.01 us
    unnamed x18 -> x6, local copies, waits for them, and re-layouts: 7.68 us -> 0.01 us
    pallas_call x1, Pallas kernels: 17.1 us -> 18 us  [exchange_gather(): pl.pallas_call(functools.partial(gather_kernel, n), out_shape=(jax.ShapeD...]
    pallas_call x1, Pallas kernels: 22.6 us -> 21.9 us  [exchange_return(): pl.pallas_call(functools.partial(return_kernel, n, scale), out_shape=(jax...]
where the time goes in v3:
time: 50.4 us; the launch traced here: 50.7 us
  Pallas kernels  49.3 us (98%)
  between operations  1.35 us (3%)
    pallas_call x1, Pallas kernels, exchange_return(): pl.pallas_call(functools.partial(return_kernel, n, scale), out_shape=(jax...  21.9 us
    pallas_call x1, Pallas kernels, exchange_gather(): pl.pallas_call(functools.partial(gather_kernel, n), out_shape=(jax.ShapeD...  18 us
    pallas_call x1, Pallas kernels, local_pass(): pl.pallas_call(local_kernel, out_shape=(jax.ShapeDtypeStruct(aggregate.sh...  7.08 us
    pallas_call x1, Pallas kernels, final_pass(): pl.pallas_call(final_kernel, out_shape=(jax.ShapeDtypeStruct(own_grad.sha...  2.31 us

profile of v3, /device:TPU:0, one launch (start us, length us, event | category | flops | bytes accessed | tf_op | source)
XLA Modules:
  0.0 50.7 jit_solution(2017470060596846793)
XLA Ops:
  1.3 0.0 copy-start
  1.3 0.0 copy-start.1
  1.3 0.0 copy-start.2
  1.3 18.0 %gather_exchange.1 = (bf16[32,16,256]{2,1,0:T(8,128)(2,1)S(1)}, s32[1,512]{1,0:T(1,128)S(1)}, s32[8,384]{1,0:T(8,128)S(1)}, bf16[256,128,128]{2,1,0:T(8,128)(2,1)S(1)}, bf16[32,128,256]{2,1,0:T(8,128)(2,1)S(1)}) custom-call(s32[1]{0:T(128)S(6)} %copy.14.tile_count, s32[1,32]{1,0:T(1,128)} %count_hbm.1, s32[16,32]{1,0:T(8,128)} %bitcast.21, ...), custom_call_target="tpu_custom_call" | custom-call | tf_op jit(solution)/shard_map/gather_exchange/pallas_call | solution.py:274
  19.3 0.0 copy-done
  19.3 0.0 copy-done.1
  19.3 0.0 copy-done.2
  19.3 7.1 %local_pass.1 = (bf16[32,128,256]{2,1,0:T(8,128)(2,1)}, bf16[33,128,256]{2,1,0:T(8,128)(2,1)S(1)}, bf16[4,128,256]{2,1,0:T(8,128)(2,1)S(1)}, bf16[8,32,256]{2,1,0:T(8,128)(2,1)S(1)}, f32[1,256]{1,0:T(1,128)S(1)}) custom-call(s32[8,384]{1,0:T(8,128)S(1)} %get-tuple-element.21.table, bf16[32,128,256]{2,1,0:T(8,128)(2,1)S(1)} %get-tuple-element.22.aggregate, ...), custom_call_target="tpu_custom_call" | custom-call | tf_op jit(solution)/shard_map/local_pass/pallas_call | solution.py:410
  26.4 21.9 %return_exchange.1 = (bf16[32,16,256]{2,1,0:T(8,128)(2,1)S(1)}, bf16[8,32,256]{2,1,0:T(8,128)(2,1)S(1)}, f32[1,256]{1,0:T(1,128)S(1)}, bf16[32,128,256]{2,1,0:T(8,128)(2,1)S(1)}) custom-call(s32[8,384]{1,0:T(8,128)S(1)} %get-tuple-element.21.table, bf16[256,128,128]{2,1,0:T(8,128)(2,1)S(1)} %get-tuple-element.24.held, ...), custom_call_target="tpu_custom_call" | custom-call | tf_op jit(solution)/shard_map/return_exchange/pallas_call | solution.py:519
  48.3 2.3 %final_pass.1 = (bf16[4096,256]{1,0:T(8,128)(2,1)}, f32[256,256]{1,0:T(8,128)}, f32[1,256]{1,0:T(1,128)}) custom-call(s32[1,512]{1,0:T(1,128)S(1)} %get-tuple-element.26.chosen_ref, bf16[512,256]{1,0:T(8,128)(2,1)S(1)} %bitcast.17, bf16[256,256]{1,0:T(8,128)(2,1)S(1)} %bitcast.18, f32[1,256]{1,0:T(1,128)S(1)} %get-tuple-element.33.bias_sum, ...), custom_call_target="tpu_custom_call" | custom-call | tf_op jit(solution)/shard_map/final_pass/pallas_call | solution.py:585
Async XLA Ops:
  1.3 18.0 %copy-start = (bf16[4096,256]{1,0:T(8,128)(2,1)S(1)}, bf16[4096,256]{1,0:T(8,128)(2,1)}, u32[]{:S(2)}) copy-start(bf16[4096,256]{1,0:T(8,128)(2,1)} %param.19) | copy-start | bytes 6291460
  1.3 18.0 %copy-start.1 = (bf16[256,256]{1,0:T(8,128)(2,1)S(1)}, bf16[256,256]{1,0:T(8,128)(2,1)}, u32[]{:S(2)}) copy-start(bf16[256,256]{1,0:T(8,128)(2,1)} %weight.1) | copy-start | bytes 393220
  1.3 18.0 %copy-start.2 = (f32[256]{0:T(256)S(1)}, f32[256]{0:T(256)}, u32[]{:S(2)}) copy-start(f32[256]{0:T(256)} %param.12) | copy-start | bytes 3076

commit v4 on v3

--- a/solution.py
+++ b/solution.py
@@ -40,7 +40,7 @@
 
 
 LANES = 128
-UNROLL = 8
+TURNS = 4
 NEAR = 8
 CHUNK = 16
 MIB = 1024 * 1024
@@ -55,11 +55,11 @@
 
 
 def pair_slots(number, keys):
-    return padded((number + keys + 1) // 2, UNROLL)
-
-
-def table_width(number, own):
-    return padded(max(2 * pair_slots(number, own), number), LANES)
+    return padded((number + keys + 1) // 2, TURNS)
+
+
+def table_width(number, ext):
+    return padded(2 * pair_slots(number, ext), LANES)
 
 
 def down(row):
@@ -116,19 +116,18 @@
 def fill_table(table, row, col, count, own, ext):
     number = row.shape[1]
     width = table.shape[1]
-    slots = pair_slots(number, own)
     used = iota((1, number), 1) < count
+    every = jnp.where(used, 1, 0)
     mine = jnp.where(used & (col < own), 1, 0)
     far = jnp.where(used & (col >= own), 1, 0)
     table[...] = jnp.zeros_like(table)
-    order, last = pair_table(row, col, mine, own, slots, width)
+    order, last = pair_table(row, col, mine, own, pair_slots(number, own), width)
     table[0:1, :] = order
     table[1:2, :LANES] = last
-    order, last = pair_table(col, row, mine, own, slots, width)
+    order, last = pair_table(col, row, every, own, pair_slots(number, ext), width)
     table[2:3, :] = order
     table[3:4, :LANES] = last
-    every = iota((number, number), 0) >= 0
-    rank = rank_of(every, far)
+    rank = rank_of(iota((number, number), 0) >= 0, far)
     low, high = bits(number), bits(ext)
     code = iota((1, number), 1) + (col + row * (1 << high)) * (1 << low)
     position = jnp.where(far > 0, rank, -1)
@@ -145,18 +144,18 @@
         wide[pl.ds(p * slots, slots), :] = jnp.broadcast_to(column, (slots, lanes))
 
 
-def run_pairs(table, line, number, zero, held, source, transposed, running, kept, begin, end):
+def run_pairs(table, line, number, zero, held, source, transposed, running, kept):
     low, high = bits(number), bits(zero + 1)
     slots = kept.shape[0] - 1
-    if begin == 0:
-        kept[slots] = jnp.zeros(kept.shape[1:], kept.dtype)
-        running[...] = jnp.zeros_like(running)
+    unroll = slots // TURNS
+    kept[slots] = jnp.zeros(kept.shape[1:], kept.dtype)
+    running[...] = jnp.zeros_like(running)
     axis = 0 if transposed else 1
 
     def turn(g, carry):
         total = running[...]
-        for j in range(UNROLL):
-            p = g * UNROLL + j
+        for j in range(unroll):
+            p = g * unroll + j
             one, two = table[line, 2 * p], table[line, 2 * p + 1]
             tiles = [held[code & ((1 << low) - 1)] for code in (one, two)]
             blocks = [source[(code >> low) & ((1 << high) - 1)] for code in (one, two)]
@@ -170,7 +169,7 @@
         running[...] = total
         return carry
 
-    lax.fori_loop(begin, end, turn, 0)
+    lax.fori_loop(0, TURNS, turn, 0)
 
 
 def gather_kernel(
@@ -203,7 +202,6 @@
     for c in range(number // chunk):
         span = pl.ds(c * chunk, chunk)
         tile_loads.append(pltpu.make_async_copy(tiles_hbm.at[span], held.at[span], tile_sem.at[c]))
-        tile_loads[c].start()
     barrier = greet(n, me)
     for copy in smalls:
         copy.wait()
@@ -218,6 +216,9 @@
             axis=1,
         )
         loads[c].wait()
+        if c == own // step - 1:
+            for load in tile_loads:
+                load.start()
         block = source[pl.ds(c * step, step)].reshape(step * edge, width)
         part = jnp.dot(hot, block, preferred_element_type=f32)
         if c == 0:
@@ -247,8 +248,7 @@
     for load in tile_loads:
         load.wait()
     move.wait()
-    turns = (kept.shape[0] - 1) // UNROLL
-    run_pairs(table, 0, number, own, held, source, False, running, kept, 0, turns)
+    run_pairs(table, 0, number, own, held, source, False, running, kept)
 
     def pick(r, carry):
         agg_ref[r] = kept[table[1, r]]
@@ -266,7 +266,7 @@
     slots = n * slot_count
     block = (n, slot_count, width)
     pairs = pair_slots(number, own)
-    table = (8, table_width(number, own))
+    table = (8, table_width(number, own + slots // edge))
     vmem = pl.BlockSpec(memory_space=VMEM)
     smem = pl.BlockSpec(memory_space=pltpu.SMEM)
     hbm = pl.BlockSpec(memory_space=pltpu.HBM)
@@ -318,58 +318,66 @@
 GROUP = 4
 
 
-def local_kernel(
-    table, aggregate, halo, held, cotangent, weight, bias,
-    activation, mixed, halo_grad, weight_part, bias_part,
-    cot, act, extra, spread, wsum, bsum, cot_sem, act_sem,
-):
-    own = aggregate.shape[0]
-    edge, width = aggregate.shape[1:]
-    number = held.shape[0]
-    far = halo.shape[0]
-    low, high = bits(number), bits(own + far)
-    step = math.gcd(own, 4)
-    steps = own // step
-    cot_copies = []
-    for b in range(steps):
-        span = pl.ds(b * step, step)
-        cot_copies.append(pltpu.make_async_copy(cotangent.at[span], cot.at[span], cot_sem.at[b]))
-        cot_copies[b].start()
+def boundary_kernel(table, halo, held, extra):
+    own = extra.shape[0] - 1
+    low, high = bits(held.shape[0]), bits(own + halo.shape[0])
 
     @pl.loop(0, own + 1)
     def _(r):
         extra[r] = jnp.zeros(extra.shape[1:], f32)
 
-    spread[...] = jnp.zeros_like(spread)
-    groups = (table[5, 0] + GROUP - 1) // GROUP
-
-    def parts(s):
-        code = table[4, s]
-        return (
-            code & ((1 << low) - 1), ((code >> low) & ((1 << high) - 1)) - own,
-            code >> (low + high),
-        )
-
-    @pl.loop(0, groups)
+    @pl.loop(0, (table[5, 0] + GROUP - 1) // GROUP)
     def _(g):
         for j in range(GROUP):
-            k, col, row = parts(g * GROUP + j)
-            extra[row] += jnp.dot(held[k], halo[col], preferred_element_type=f32)
-
+            code = table[4, g * GROUP + j]
+            col = ((code >> low) & ((1 << high) - 1)) - own
+            extra[code >> (low + high)] += jnp.dot(
+                held[code & ((1 << low) - 1)], halo[col], preferred_element_type=f32
+            )
+
+
+def boundary_pass(own, table, halo, held):
+    edge, width = halo.shape[1:]
+    vmem = pl.BlockSpec(memory_space=VMEM)
+    return pl.pallas_call(
+        boundary_kernel,
+        out_shape=jax.ShapeDtypeStruct((own + 1, edge, width), f32),
+        in_specs=[pl.BlockSpec(memory_space=pltpu.SMEM), vmem, vmem],
+        out_specs=vmem,
+        compiler_params=pltpu.CompilerParams(vmem_limit_bytes=4 * MIB),
+        name="boundary_pass",
+    )(table, halo, held)
+
+
+def return_kernel(
+    n, near, slot_count, scale,
+    table_ref, held, aggregate, extra, cot, weight, bias,
+    halo_in, pieces_in, bsum_ref, own_grad, act,
+    table, mixed, wsum, bsum, halo_ref, halo_land, weight_ref, near_in, mine, far_in, piece,
+    pieces_land, bias_ref, bias_near, bias_mine, bias_far, running, kept,
+    halo_s, halo_r, near_s, near_r, far_s, far_r, piece_s, piece_r,
+    bias_near_s, bias_near_r, bias_far_s, bias_far_r, table_sem,
+):
+    me = lax.axis_index("dom")
+    move = pltpu.make_async_copy(table_ref, table, table_sem)
+    move.start()
+    barrier = greet(n, me)
+    far = n // near
+    block, seat = lax.div(me, near), lax.rem(me, near)
+    number = held.shape[0]
+    own, edge, width = aggregate.shape
+    step = math.gcd(own, 4)
     wsum[...] = jnp.zeros_like(wsum)
     bsum[...] = jnp.zeros_like(bsum)
-    act_copies = []
-    for b in range(steps):
+
+    def activate(b, carry):
         span = pl.ds(b * step, step)
-        act_copies.append(pltpu.make_async_copy(act.at[span], activation.at[span], act_sem.at[b]))
         agg = (aggregate[span].astype(f32) + extra[span]).astype(bf16).reshape(step * edge, width)
         linear = jnp.dot(agg, weight[...], preferred_element_type=f32) + bias[...]
         sig = 0.5 * jnp.tanh(0.5 * linear) + 0.5
         value = linear * sig
         act[span] = value.astype(bf16).reshape(step, edge, width)
-        act_copies[b].start()
         slope = sig + value * (1.0 - sig)
-        cot_copies[b].wait()
         grad = (cot[span].reshape(step * edge, width).astype(f32) * slope).astype(bf16)
         wsum[...] += lax.dot_general(
             agg, grad, (((0,), (0,)), ((), ())), preferred_element_type=f32
@@ -379,79 +387,13 @@
             grad, weight[...], (((1,), (1,)), ((), ())), preferred_element_type=f32
         )
         mixed[span] = back.astype(bf16).reshape(step, edge, width)
+        return carry
+
+    lax.fori_loop(0, own // step, activate, 0, unroll=True)
     mixed[own] = jnp.zeros((edge, width), bf16)
-
-    @pl.loop(0, groups)
-    def _(g):
-        for j in range(GROUP):
-            s = g * GROUP + j
-            k, col, row = parts(s)
-            target = jnp.where(s < table[5, 0], col, far)
-            spread[target] += lax.dot_general(
-                held[k], mixed[row], (((0,), (0,)), ((), ())), preferred_element_type=f32
-            )
-
-    halo_grad[...] = spread[pl.ds(0, far)].astype(bf16)
-    pieces, piece_rows = weight_part.shape[:2]
-    for p in range(pieces):
-        weight_part[p] = wsum[pl.ds(p * piece_rows, piece_rows), :].astype(bf16)
-    bias_part[...] = bsum[...]
-    for copy in act_copies:
-        copy.wait()
-
-
-def local_pass(near, table, aggregate, halo, held, cotangent, weight, bias):
-    own, edge, width = aggregate.shape
-    steps = own // math.gcd(own, 4)
-    hbm = pl.BlockSpec(memory_space=pltpu.HBM)
-    smem = pl.BlockSpec(memory_space=pltpu.SMEM)
-    vmem = pl.BlockSpec(memory_space=VMEM)
-    dma = pltpu.SemaphoreType.DMA
-    return pl.pallas_call(
-        local_kernel,
-        out_shape=(
-            jax.ShapeDtypeStruct(aggregate.shape, bf16),
-            jax.ShapeDtypeStruct((own + 1, edge, width), bf16),
-            jax.ShapeDtypeStruct(halo.shape, bf16),
-            jax.ShapeDtypeStruct((near, width // near, width), bf16),
-            jax.ShapeDtypeStruct((1, width), f32),
-        ),
-        in_specs=[smem, vmem, vmem, vmem, hbm, vmem, vmem],
-        out_specs=(hbm, vmem, vmem, vmem, vmem),
-        scratch_shapes=[
-            VMEM(aggregate.shape, bf16),
-            VMEM(aggregate.shape, bf16),
-            VMEM((own + 1, edge, width), f32),
-            VMEM((halo.shape[0] + 1, edge, width), f32),
-            VMEM((width, width), f32),
-            VMEM((1, width), f32),
-            dma((steps,)),
-            dma((steps,)),
-        ],
-        compiler_params=pltpu.CompilerParams(vmem_limit_bytes=24 * MIB + halo.size * 16),
-        name="local_pass",
-    )(table, aggregate, halo, held, cotangent, weight, bias)
-
-
-def return_kernel(
-    n, scale, table, held, mixed, halo_ref, weight_ref, bias_ref,
-    halo_in, pieces_in, bsum_ref, own_grad,
-    halo_land, bias_in, near_in, mine, far_in, piece, pieces_land, running, kept,
-    halo_s, halo_r, bias_s, bias_r, near_s, near_r, far_s, far_r, piece_s, piece_r,
-):
-    me = lax.axis_index("dom")
-    barrier = greet(n, me)
-    near = weight_ref.shape[0]
-    far = n // near
-    block, seat = lax.div(me, near), lax.rem(me, near)
-    number = held.shape[0]
-    own = mixed.shape[0] - 1
-    turns = (kept.shape[0] - 1) // UNROLL
-    early = turns // 3
-    pairs = functools.partial(run_pairs, table, 2, number, own, held, mixed, True, running, kept)
-    pairs(0, early)
+    weight_ref[...] = wsum[...].astype(bf16).reshape(weight_ref.shape)
+    bias_ref[...] = bsum[...]
     halo_copy = functools.partial(push, n, me, lambda p: halo_ref.at[p], halo_land, halo_s, halo_r)
-    bias_copy = functools.partial(push, n, me, lambda p: bias_ref, bias_in, bias_s, bias_r)
 
     def inside(src, dst, send_sem, recv_sem, i):
         peer = lax.rem(seat + i, near)
@@ -460,15 +402,18 @@
             recv_sem=recv_sem.at[i], device_id=(block * near + peer,), device_id_type=MESH,
         )
 
-    def across(i):
+    def across(src, dst, send_sem, recv_sem, i):
         peer = lax.rem(block + i, far)
         return pltpu.make_async_remote_copy(
-            src_ref=mine, dst_ref=far_in.at[block], send_sem=far_s.at[i],
-            recv_sem=far_r.at[i], device_id=(peer * near + seat,), device_id_type=MESH,
+            src_ref=src, dst_ref=dst.at[block], send_sem=send_sem.at[i],
+            recv_sem=recv_sem.at[i], device_id=(peer * near + seat,), device_id_type=MESH,
         )
 
     near_copy = functools.partial(inside, lambda p: weight_ref.at[p], near_in, near_s, near_r)
     piece_copy = functools.partial(inside, lambda p: piece, pieces_land, piece_s, piece_r)
+    bias_one = functools.partial(inside, lambda p: bias_ref, bias_near, bias_near_s, bias_near_r)
+    far_copy = functools.partial(across, mine, far_in, far_s, far_r)
+    bias_two = functools.partial(across, bias_mine, bias_far, bias_far_s, bias_far_r)
 
     def over(count, step):
         def turn(i, carry):
@@ -479,79 +424,107 @@
 
     pl.semaphore_wait(barrier, n - 1)
     over(near, lambda i: near_copy(i).start())
-    over(n, lambda i: halo_copy(i).start())
-    over(n, lambda i: bias_copy(i).start())
+    over(near, lambda i: bias_one(i).start())
     near_in[seat] = weight_ref[seat]
-    bias_in[me] = bias_ref[...]
-    halo_land[me] = halo_ref[me]
-    pairs(early, turns)
+    bias_near[seat] = bias_ref[...]
+    move.wait()
+    run_pairs(table, 2, number, own, held, mixed, True, running, kept)
+    each = edge // slot_count
+
+    def load(b, carry):
+        halo_ref[pl.ds(b * each, each)] = kept[table[3, own + b]].reshape(each, slot_count, width)
+        return carry
+
+    lax.fori_loop(0, n // each, load, 0)
     over(near, lambda i: near_copy(i).wait())
     mine[...] = jnp.sum(near_in[...].astype(f32), axis=0).astype(bf16)
-    over(far, lambda i: across(i).start())
+    over(far, lambda i: far_copy(i).start())
+    over(n, lambda i: halo_copy(i).start())
+    halo_land[me] = halo_ref[me]
+    over(near, lambda i: bias_one(i).wait())
+    bias_mine[...] = jnp.sum(bias_near[...], axis=0)
+    over(far, lambda i: bias_two(i).start())
     far_in[block] = mine[...]
+    bias_far[block] = bias_mine[...]
 
     def pick(c, carry):
         own_grad[c] = kept[table[3, c]]
         return carry
 
     lax.fori_loop(0, own, pick, 0)
-    over(far, lambda i: across(i).wait())
+    over(far, lambda i: far_copy(i).wait())
     piece[...] = (jnp.sum(far_in[...].astype(f32), axis=0) * scale).astype(bf16)
     over(near, lambda i: piece_copy(i).start())
     pieces_land[seat] = piece[...]
-    over(n, lambda i: bias_copy(i).wait())
-    bsum_ref[...] = jnp.sum(bias_in[...], axis=0) * scale
+    over(far, lambda i: bias_two(i).wait())
+    bsum_ref[...] = jnp.sum(bias_far[...], axis=0) * scale
     over(n, lambda i: halo_copy(i).wait())
     halo_in[...] = halo_land[...]
     over(near, lambda i: piece_copy(i).wait())
     pieces_in[...] = pieces_land[...]
 
 
-def exchange_return(n, scale, table, held, mixed, halo_grad, weight_part, bias_part):
+def exchange_return(
+    n, slot_count, scale, table, held, aggregate, extra, cotangent, weight, bias
+):
     vmem = pl.BlockSpec(memory_space=VMEM)
-    smem = pl.BlockSpec(memory_space=pltpu.SMEM)
     dma = pltpu.SemaphoreType.DMA
-    edge, width = mixed.shape[1:]
-    own = mixed.shape[0] - 1
-    pairs = pair_slots(held.shape[0], own)
-    near = weight_part.shape[0]
-    piece = weight_part.shape[1:]
+    own, edge, width = aggregate.shape
+    number = held.shape[0]
+    ext = own + n * slot_count // edge
+    pairs = pair_slots(number, ext)
+    near = math.gcd(n, NEAR)
+    far = n // near
+    block = (n, slot_count, width)
+    piece = (width // near, width)
     return pl.pallas_call(
-        functools.partial(return_kernel, n, scale),
+        functools.partial(return_kernel, n, near, slot_count, scale),
         out_shape=(
-            jax.ShapeDtypeStruct(halo_grad.shape, bf16),
-            jax.ShapeDtypeStruct(weight_part.shape, bf16),
-            jax.ShapeDtypeStruct(bias_part.shape, f32),
+            jax.ShapeDtypeStruct(block, bf16),
+            jax.ShapeDtypeStruct((near,) + piece, bf16),
+            jax.ShapeDtypeStruct((1, width), f32),
+            jax.ShapeDtypeStruct((own, edge, width), bf16),
             jax.ShapeDtypeStruct((own, edge, width), bf16),
         ),
-        in_specs=[smem] + [vmem] * 5,
-        out_specs=(vmem,) * 4,
+        in_specs=[vmem] * 7,
+        out_specs=(vmem,) * 5,
         scratch_shapes=[
-            VMEM(halo_grad.shape, bf16),
-            VMEM((n,) + bias_part.shape, f32),
-            VMEM(weight_part.shape, bf16),
+            pltpu.SMEM(table.shape, jnp.int32),
+            VMEM((own + 1, edge, width), bf16),
+            VMEM((width, width), f32),
+            VMEM((1, width), f32),
+            VMEM(block, bf16),
+            VMEM(block, bf16),
+            VMEM((near,) + piece, bf16),
+            VMEM((near,) + piece, bf16),
             VMEM(piece, bf16),
-            VMEM((n // near,) + piece, bf16),
+            VMEM((far,) + piece, bf16),
             VMEM(piece, bf16),
-            VMEM(weight_part.shape, bf16),
+            VMEM((near,) + piece, bf16),
+            VMEM((1, width), f32),
+            VMEM((near, 1, width), f32),
+            VMEM((1, width), f32),
+            VMEM((far, 1, width), f32),
             VMEM((edge, width), f32),
             VMEM((pairs + 1, edge, width), bf16),
         ]
-        + [dma((n,))] * 4
+        + [dma((n,))] * 2
         + [dma((near,))] * 2
-        + [dma((n // near,))] * 2
-        + [dma((near,))] * 2,
+        + [dma((far,))] * 2
+        + [dma((near,))] * 4
+        + [dma((far,))] * 2
+        + [dma],
         compiler_params=pltpu.CompilerParams(
             collective_id=1, has_side_effects=True,
-            vmem_limit_bytes=20 * MIB + halo_grad.size * 16,
+            vmem_limit_bytes=20 * MIB + n * slot_count * width * 16,
         ),
         name="return_exchange",
-    )(table, held, mixed, halo_grad, weight_part, bias_part)
+    )(table, held, aggregate, extra, cotangent, weight, bias)
 
 
 def final_kernel(
-    chosen_ref, returned, pieces, bias_sum, own, out_hbm, wsum_hbm, bsum_hbm,
-    out, wsum, bsum, out_sem, small_sem,
+    chosen_ref, returned, pieces, bias_sum, own, act, out_hbm, wsum_hbm, bsum_hbm, act_hbm,
+    out, wsum, bsum, out_sem, act_sem, small_sem,
 ):
     rows = own.shape[0]
     step = math.gcd(rows, 512)
@@ -561,6 +534,10 @@
     outs = [
         pltpu.make_async_copy(wsum, wsum_hbm, small_sem.at[0]),
         pltpu.make_async_copy(bsum, bsum_hbm, small_sem.at[1]),
+    ]
+    outs += [
+        pltpu.make_async_copy(act.at[span], act_hbm.at[span], act_sem.at[c])
+        for c, span in enumerate(spans)
     ]
     for copy in outs:
         copy.start()
@@ -577,7 +554,7 @@
         copy.wait()
 
 
-def final_pass(chosen, returned, pieces, bias_sum, own_grad):
+def final_pass(chosen, returned, pieces, bias_sum, own_grad, activation):
     rows, width = own_grad.shape
     vmem = pl.BlockSpec(memory_space=VMEM)
     hbm = pl.BlockSpec(memory_space=pltpu.HBM)
@@ -588,19 +565,21 @@
             jax.ShapeDtypeStruct(own_grad.shape, bf16),
             jax.ShapeDtypeStruct(pieces.shape, f32),
             jax.ShapeDtypeStruct(bias_sum.shape, f32),
+            jax.ShapeDtypeStruct(activation.shape, bf16),
         ),
-        in_specs=[vmem] * 5,
-        out_specs=(hbm,) * 3,
+        in_specs=[vmem] * 6,
+        out_specs=(hbm,) * 4,
         scratch_shapes=[
             VMEM(own_grad.shape, bf16),
             VMEM(pieces.shape, f32),
             VMEM(bias_sum.shape, f32),
             pltpu.SemaphoreType.DMA((steps,)),
+            pltpu.SemaphoreType.DMA((steps,)),
             pltpu.SemaphoreType.DMA((2,)),
         ],
         compiler_params=pltpu.CompilerParams(vmem_limit_bytes=12 * MIB + returned.size * 32),
         name="final_pass",
-    )(chosen, returned, pieces, bias_sum, own_grad)
+    )(chosen, returned, pieces, bias_sum, own_grad, activation)
 
 
 def body(
@@ -617,20 +596,17 @@
     halo, chosen, table, held, aggregate = exchange_gather(
         n, send_count, tile_count, send_rows, tile_row, tile_col, blocks(features), tile_values
     )
-    activation, mixed, halo_grad, weight_part, bias_part = local_pass(
-        math.gcd(n, NEAR), table, aggregate, blocks(halo), held, blocks(cotangent), weight,
+    extra = boundary_pass(rows // edge, table, blocks(halo), held)
+    scale = float(rows * n) ** (-0.5)
+    returned, pieces, bias_sum, own_grad, activation = exchange_return(
+        n, slot_count, scale, table, held, aggregate, extra, blocks(cotangent), weight,
         bias_vector.reshape(1, width),
     )
-    scale = float(rows * n) ** (-0.5)
-    returned, pieces, bias_sum, own_grad = exchange_return(
-        n, scale, table, held, mixed, halo_grad.reshape(n, slot_count, width), weight_part,
-        bias_part,
+    grad_features, weight_sum, bias_sum, activation = final_pass(
+        chosen, returned.reshape(slots, width), pieces.reshape(width, width), bias_sum,
+        own_grad.reshape(rows, width), activation.reshape(rows, width),
     )
-    grad_features, weight_sum, bias_sum = final_pass(
-        chosen, returned.reshape(slots, width), pieces.reshape(width, width), bias_sum,
-        own_grad.reshape(rows, width),
-    )
-    return (activation.reshape(rows, width), grad_features, weight_sum, bias_sum.reshape(width))
+    return (activation, grad_features, weight_sum, bias_sum.reshape(width))
 
 
 def solution(mesh):

time: 50.4 us -> 41.7 us (0.83)
  Pallas kernels: 49.3 us -> 40.1 us
    pallas_call x2, Pallas kernels: 29 us -> 21.6 us  [the longest x1 19.6 us: exchange_return(): pl.pallas_call(functools.partial(return_kernel, n, near, slot_count, scal...]
    pallas_call x1, Pallas kernels: 18 us -> 15.6 us  [exchange_gather(): pl.pallas_call(functools.partial(gather_kernel, n), out_shape=(jax.ShapeD...]
    pallas_call x1, Pallas kernels: 2.31 us -> 2.99 us  [final_pass(): pl.pallas_call(final_kernel, out_shape=(jax.ShapeDtypeStruct(own_grad.sha...]
where the time goes in v4:
time: 41.7 us; the launch traced here: 41.5 us
  Pallas kernels  40.1 us (96%)
  between operations  1.35 us (3%)
    pallas_call x1, Pallas kernels, exchange_return(): pl.pallas_call(functools.partial(return_kernel, n, near, slot_count, scal...  19.6 us
    pallas_call x1, Pallas kernels, exchange_gather(): pl.pallas_call(functools.partial(gather_kernel, n), out_shape=(jax.ShapeD...  15.6 us
    pallas_call x1, Pallas kernels, final_pass(): pl.pallas_call(final_kernel, out_shape=(jax.ShapeDtypeStruct(own_grad.sha...  2.99 us
    pallas_call x1, Pallas kernels, boundary_pass(): pl.pallas_call(boundary_kernel, out_shape=jax.ShapeDtypeStruct((own + 1,...  2 us

profile of v4, /device:TPU:0, one launch (start us, length us, event | category | flops | bytes accessed | tf_op | source)
XLA Modules:
  0.0 41.5 jit_solution(2332988349823223048)
XLA Ops:
  1.3 15.6 %gather_exchange.1 = (bf16[32,16,256]{2,1,0:T(8,128)(2,1)S(1)}, s32[1,512]{1,0:T(1,128)S(1)}, s32[8,384]{1,0:T(8,128)S(1)}, bf16[256,128,128]{2,1,0:T(8,128)(2,1)S(1)}, bf16[32,128,256]{2,1,0:T(8,128)(2,1)S(1)}) custom-call(s32[1]{0:T(128)S(6)} %copy.14.tile_count, s32[1,32]{1,0:T(1,128)} %count_hbm.1, s32[16,32]{1,0:T(8,128)} %bitcast.20, ...), custom_call_target="tpu_custom_call" | custom-call | tf_op jit(solution)/shard_map/gather_exchange/pallas_call | solution.py:274
  16.9 0.0 copy-start
  16.9 0.0 copy-start.1
  16.9 0.0 copy-start.2
  16.9 2.0 %boundary_pass.1.extra = f32[33,128,256]{2,1,0:T(8,128)S(1)} custom-call(s32[8,384]{1,0:T(8,128)S(1)} %get-tuple-element.19.table.table_ref, bf16[4,128,256]{2,1,0:T(8,128)(2,1)S(1)} %bitcast.16, bf16[256,128,128]{2,1,0:T(8,128)(2,1)S(1)} %get-tuple-element.20.held), custom_call_target="tpu_custom_call" | custom-call | tf_op jit(solution)/shard_map/boundary_pass/pallas_call | solution.py:342
  18.9 0.0 copy-done
  18.9 0.0 copy-done.1
  18.9 0.0 copy-done.2
  18.9 19.6 %return_exchange.1 = (bf16[32,16,256]{2,1,0:T(8,128)(2,1)S(1)}, bf16[8,32,256]{2,1,0:T(8,128)(2,1)S(1)}, f32[1,256]{1,0:T(1,128)S(1)}, bf16[32,128,256]{2,1,0:T(8,128)(2,1)S(1)}, bf16[32,128,256]{2,1,0:T(8,128)(2,1)S(1)}) custom-call(s32[8,384]{1,0:T(8,128)S(1)} %get-tuple-element.19.table.table_ref, bf16[256,128,128]{2,1,0:T(8,128)(2,1)S(1)} %get-tuple-element.20.held, ...), custom_call_target="tpu_custom_call" | custom-call | tf_op jit(solution)/shard_map/return_exchange/pallas_call | solution.py:480
  38.5 3.0 %final_pass.1 = (bf16[4096,256]{1,0:T(8,128)(2,1)}, f32[256,256]{1,0:T(8,128)}, f32[1,256]{1,0:T(1,128)}, bf16[4096,256]{1,0:T(8,128)(2,1)}) custom-call(s32[1,512]{1,0:T(1,128)S(1)} %get-tuple-element.18.chosen_ref, bf16[512,256]{1,0:T(8,128)(2,1)S(1)} %bitcast.15, bf16[256,256]{1,0:T(8,128)(2,1)S(1)} %bitcast.17, f32[1,256]{1,0:T(1,128)S(1)} %get-tuple-element.25.bias_sum, ...), custom_call_target="tpu_custom_call" | custom-call | tf_op jit(solution)/shard_map/final_pass/pallas_call | solution.py:562
Async XLA Ops:
  16.9 2.1 %copy-start = (bf16[4096,256]{1,0:T(8,128)(2,1)S(1)}, bf16[4096,256]{1,0:T(8,128)(2,1)}, u32[]{:S(2)}) copy-start(bf16[4096,256]{1,0:T(8,128)(2,1)} %param.19) | copy-start | bytes 6291460
  16.9 2.0 %copy-start.1 = (bf16[256,256]{1,0:T(8,128)(2,1)S(1)}, bf16[256,256]{1,0:T(8,128)(2,1)}, u32[]{:S(2)}) copy-start(bf16[256,256]{1,0:T(8,128)(2,1)} %weight.1) | copy-start | bytes 393220
  16.9 2.0 %copy-start.2 = (f32[256]{0:T(256)S(1)}, f32[256]{0:T(256)}, u32[]{:S(2)}) copy-start(f32[256]{0:T(256)} %param.12) | copy-start | bytes 3076

commit v5 on v4

--- a/solution.py
+++ b/solution.py
@@ -40,7 +40,7 @@
 
 
 LANES = 128
-TURNS = 4
+TURNS = 2
 NEAR = 8
 CHUNK = 16
 MIB = 1024 * 1024
@@ -315,7 +315,7 @@
     )
 
 
-GROUP = 4
+GROUP = 16
 
 
 def boundary_kernel(table, halo, held, extra):
@@ -349,14 +349,22 @@
     )(table, halo, held)
 
 
+SPLIT = 8
+
+
+def split(total):
+    upper = total.astype(bf16).astype(f32)
+    row = iota((SPLIT, total.shape[1]), 0)
+    return jnp.where(row == 0, upper, jnp.where(row == 1, total - upper, 0.0)).astype(bf16)
+
+
 def return_kernel(
     n, near, slot_count, scale,
     table_ref, held, aggregate, extra, cot, weight, bias,
     halo_in, pieces_in, bsum_ref, own_grad, act,
     table, mixed, wsum, bsum, halo_ref, halo_land, weight_ref, near_in, mine, far_in, piece,
-    pieces_land, bias_ref, bias_near, bias_mine, bias_far, running, kept,
-    halo_s, halo_r, near_s, near_r, far_s, far_r, piece_s, piece_r,
-    bias_near_s, bias_near_r, bias_far_s, bias_far_r, table_sem,
+    pieces_land, running, kept,
+    halo_s, halo_r, near_s, near_r, far_s, far_r, piece_s, piece_r, table_sem,
 ):
     me = lax.axis_index("dom")
     move = pltpu.make_async_copy(table_ref, table, table_sem)
@@ -391,8 +399,9 @@
 
     lax.fori_loop(0, own // step, activate, 0, unroll=True)
     mixed[own] = jnp.zeros((edge, width), bf16)
-    weight_ref[...] = wsum[...].astype(bf16).reshape(weight_ref.shape)
-    bias_ref[...] = bsum[...]
+    rows = piece.shape[0]
+    weight_ref[:, :rows, :] = wsum[...].astype(bf16).reshape(near, rows, width)
+    weight_ref[:, rows:, :] = jnp.broadcast_to(split(bsum[...])[None], (near, SPLIT, width))
     halo_copy = functools.partial(push, n, me, lambda p: halo_ref.at[p], halo_land, halo_s, halo_r)
 
     def inside(src, dst, send_sem, recv_sem, i):
@@ -411,9 +420,7 @@
 
     near_copy = functools.partial(inside, lambda p: weight_ref.at[p], near_in, near_s, near_r)
     piece_copy = functools.partial(inside, lambda p: piece, pieces_land, piece_s, piece_r)
-    bias_one = functools.partial(inside, lambda p: bias_ref, bias_near, bias_near_s, bias_near_r)
     far_copy = functools.partial(across, mine, far_in, far_s, far_r)
-    bias_two = functools.partial(across, bias_mine, bias_far, bias_far_s, bias_far_r)
 
     def over(count, step):
         def turn(i, carry):
@@ -424,9 +431,7 @@
 
     pl.semaphore_wait(barrier, n - 1)
     over(near, lambda i: near_copy(i).start())
-    over(near, lambda i: bias_one(i).start())
     near_in[seat] = weight_ref[seat]
-    bias_near[seat] = bias_ref[...]
     move.wait()
     run_pairs(table, 2, number, own, held, mixed, True, running, kept)
     each = edge // slot_count
@@ -437,15 +442,13 @@
 
     lax.fori_loop(0, n // each, load, 0)
     over(near, lambda i: near_copy(i).wait())
-    mine[...] = jnp.sum(near_in[...].astype(f32), axis=0).astype(bf16)
+    summed = jnp.sum(near_in[...].astype(f32), axis=0)
+    mine[:rows, :] = summed[:rows].astype(bf16)
+    mine[rows:, :] = split(summed[rows : rows + 1] + summed[rows + 1 : rows + 2])
     over(far, lambda i: far_copy(i).start())
     over(n, lambda i: halo_copy(i).start())
     halo_land[me] = halo_ref[me]
-    over(near, lambda i: bias_one(i).wait())
-    bias_mine[...] = jnp.sum(bias_near[...], axis=0)
-    over(far, lambda i: bias_two(i).start())
     far_in[block] = mine[...]
-    bias_far[block] = bias_mine[...]
 
     def pick(c, carry):
         own_grad[c] = kept[table[3, c]]
@@ -453,11 +456,11 @@
 
     lax.fori_loop(0, own, pick, 0)
     over(far, lambda i: far_copy(i).wait())
-    piece[...] = (jnp.sum(far_in[...].astype(f32), axis=0) * scale).astype(bf16)
+    summed = jnp.sum(far_in[...].astype(f32), axis=0) * scale
+    piece[...] = summed[:rows].astype(bf16)
     over(near, lambda i: piece_copy(i).start())
     pieces_land[seat] = piece[...]
-    over(far, lambda i: bias_two(i).wait())
-    bsum_ref[...] = jnp.sum(bias_far[...], axis=0) * scale
+    bsum_ref[...] = summed[rows : rows + 1] + summed[rows + 1 : rows + 2]
     over(n, lambda i: halo_copy(i).wait())
     halo_in[...] = halo_land[...]
     over(near, lambda i: piece_copy(i).wait())
@@ -477,6 +480,7 @@
     far = n // near
     block = (n, slot_count, width)
     piece = (width // near, width)
+    longer = (piece[0] + SPLIT, width)
     return pl.pallas_call(
         functools.partial(return_kernel, n, near, slot_count, scale),
         out_shape=(
@@ -495,24 +499,19 @@
             VMEM((1, width), f32),
             VMEM(block, bf16),
             VMEM(block, bf16),
-            VMEM((near,) + piece, bf16),
-            VMEM((near,) + piece, bf16),
-            VMEM(piece, bf16),
-            VMEM((far,) + piece, bf16),
+            VMEM((near,) + longer, bf16),
+            VMEM((near,) + longer, bf16),
+            VMEM(longer, bf16),
+            VMEM((far,) + longer, bf16),
             VMEM(piece, bf16),
             VMEM((near,) + piece, bf16),
-            VMEM((1, width), f32),
-            VMEM((near, 1, width), f32),
-            VMEM((1, width), f32),
-            VMEM((far, 1, width), f32),
             VMEM((edge, width), f32),
             VMEM((pairs + 1, edge, width), bf16),
         ]
         + [dma((n,))] * 2
         + [dma((near,))] * 2
         + [dma((far,))] * 2
-        + [dma((near,))] * 4
-        + [dma((far,))] * 2
+        + [dma((near,))] * 2
         + [dma],
         compiler_params=pltpu.CompilerParams(
             collective_id=1, has_side_effects=True,

time: 41.7 us -> 39.6 us (0.950)
  Pallas kernels: 40.1 us -> 37.7 us
    pallas_call x1, Pallas kernels: 19.6 us -> 17.2 us  [exchange_return(): pl.pallas_call(functools.partial(return_kernel, n, near, slot_count, scal...]
where the time goes in v5:
time: 39.6 us; the launch traced here: 39.1 us
  Pallas kernels  37.7 us (95%)
  between operations  1.35 us (3%)
    pallas_call x1, Pallas kernels, exchange_return(): pl.pallas_call(functools.partial(return_kernel, n, near, slot_count, scal...  17.2 us
    pallas_call x1, Pallas kernels, exchange_gather(): pl.pallas_call(functools.partial(gather_kernel, n), out_shape=(jax.ShapeD...  15.6 us
    pallas_call x1, Pallas kernels, final_pass(): pl.pallas_call(final_kernel, out_shape=(jax.ShapeDtypeStruct(own_grad.sha...  2.98 us
    pallas_call x1, Pallas kernels, boundary_pass(): pl.pallas_call(boundary_kernel, out_shape=jax.ShapeDtypeStruct((own + 1,...  1.98 us

profile of v5, /device:TPU:0, one launch (start us, length us, event | category | flops | bytes accessed | tf_op | source)
XLA Modules:
  0.0 39.1 jit_solution(1671555939942855335)
XLA Ops:
  1.3 15.6 %gather_exchange.1 = (bf16[32,16,256]{2,1,0:T(8,128)(2,1)S(1)}, s32[1,512]{1,0:T(1,128)S(1)}, s32[8,384]{1,0:T(8,128)S(1)}, bf16[256,128,128]{2,1,0:T(8,128)(2,1)S(1)}, bf16[32,128,256]{2,1,0:T(8,128)(2,1)S(1)}) custom-call(s32[1]{0:T(128)S(6)} %copy.14.tile_count, s32[1,32]{1,0:T(1,128)} %count_hbm.1, s32[16,32]{1,0:T(8,128)} %bitcast.20, ...), custom_call_target="tpu_custom_call" | custom-call | tf_op jit(solution)/shard_map/gather_exchange/pallas_call | solution.py:274
  16.9 0.0 copy-start
  16.9 0.0 copy-start.1
  16.9 0.0 copy-start.2
  16.9 2.0 %boundary_pass.1.extra = f32[33,128,256]{2,1,0:T(8,128)S(1)} custom-call(s32[8,384]{1,0:T(8,128)S(1)} %get-tuple-element.19.table.table_ref, bf16[4,128,256]{2,1,0:T(8,128)(2,1)S(1)} %bitcast.16, bf16[256,128,128]{2,1,0:T(8,128)(2,1)S(1)} %get-tuple-element.20.held), custom_call_target="tpu_custom_call" | custom-call | tf_op jit(solution)/shard_map/boundary_pass/pallas_call | solution.py:342
  18.9 0.0 copy-done
  18.9 0.0 copy-done.1
  18.9 0.0 copy-done.2
  18.9 17.2 %return_exchange.1 = (bf16[32,16,256]{2,1,0:T(8,128)(2,1)S(1)}, bf16[8,32,256]{2,1,0:T(8,128)(2,1)S(1)}, f32[1,256]{1,0:T(1,128)S(1)}, bf16[32,128,256]{2,1,0:T(8,128)(2,1)S(1)}, bf16[32,128,256]{2,1,0:T(8,128)(2,1)S(1)}) custom-call(s32[8,384]{1,0:T(8,128)S(1)} %get-tuple-element.19.table.table_ref, bf16[256,128,128]{2,1,0:T(8,128)(2,1)S(1)} %get-tuple-element.20.held, ...), custom_call_target="tpu_custom_call" | custom-call | tf_op jit(solution)/shard_map/return_exchange/pallas_call | solution.py:484
  36.1 3.0 %final_pass.1 = (bf16[4096,256]{1,0:T(8,128)(2,1)}, f32[256,256]{1,0:T(8,128)}, f32[1,256]{1,0:T(1,128)}, bf16[4096,256]{1,0:T(8,128)(2,1)}) custom-call(s32[1,512]{1,0:T(1,128)S(1)} %get-tuple-element.18.chosen_ref, bf16[512,256]{1,0:T(8,128)(2,1)S(1)} %bitcast.15, bf16[256,256]{1,0:T(8,128)(2,1)S(1)} %bitcast.17, f32[1,256]{1,0:T(1,128)S(1)} %get-tuple-element.25.bias_sum, ...), custom_call_target="tpu_custom_call" | custom-call | tf_op jit(solution)/shard_map/final_pass/pallas_call | solution.py:561
Async XLA Ops:
  16.9 2.0 %copy-start = (bf16[4096,256]{1,0:T(8,128)(2,1)S(1)}, bf16[4096,256]{1,0:T(8,128)(2,1)}, u32[]{:S(2)}) copy-start(bf16[4096,256]{1,0:T(8,128)(2,1)} %param.19) | copy-start | bytes 6291460
  16.9 2.0 %copy-start.1 = (bf16[256,256]{1,0:T(8,128)(2,1)S(1)}, bf16[256,256]{1,0:T(8,128)(2,1)}, u32[]{:S(2)}) copy-start(bf16[256,256]{1,0:T(8,128)(2,1)} %weight.1) | copy-start | bytes 393220
  16.9 2.0 %copy-start.2 = (f32[256]{0:T(256)S(1)}, f32[256]{0:T(256)}, u32[]{:S(2)}) copy-start(f32[256]{0:T(256)} %param.12) | copy-start | bytes 3076

commit v6 on v5

--- a/solution.py
+++ b/solution.py
@@ -173,11 +173,11 @@
 
 
 def gather_kernel(
-    n, tile_count, count_hbm, rows_hbm, row_hbm, col_hbm, features_hbm, tiles_hbm,
-    halo_ref, chosen_ref, table_ref, held, agg_ref,
+    n, tile_count, count_hbm, rows_hbm, row_hbm, col_hbm, features_hbm, tiles_hbm, cot_hbm,
+    halo_ref, chosen_ref, table_ref, held, agg_ref, extra_ref, cot_ref,
     count_ref, rows_ref, row_ref, col_ref,
     source, wide, total, sent, landed, table, running, kept,
-    send_sem, recv_sem, load_sem, tile_sem, table_sem, small_sem,
+    send_sem, recv_sem, load_sem, tile_sem, table_sem, small_sem, cot_sem,
 ):
     me = lax.axis_index("dom")
     own = features_hbm.shape[0]
@@ -202,6 +202,7 @@
     for c in range(number // chunk):
         span = pl.ds(c * chunk, chunk)
         tile_loads.append(pltpu.make_async_copy(tiles_hbm.at[span], held.at[span], tile_sem.at[c]))
+    cot_load = pltpu.make_async_copy(cot_hbm, cot_ref, cot_sem)
     barrier = greet(n, me)
     for copy in smalls:
         copy.wait()
@@ -219,6 +220,7 @@
         if c == own // step - 1:
             for load in tile_loads:
                 load.start()
+            cot_load.start()
         block = source[pl.ds(c * step, step)].reshape(step * edge, width)
         part = jnp.dot(hot, block, preferred_element_type=f32)
         if c == 0:
@@ -252,14 +254,18 @@
 
     def pick(r, carry):
         agg_ref[r] = kept[table[1, r]]
+        extra_ref[r] = jnp.zeros(extra_ref.shape[1:], f32)
         return carry
 
     lax.fori_loop(0, own, pick, 0)
+    cot_load.wait()
     lax.fori_loop(1, n, finish, 0)
     halo_ref[...] = landed[...]
 
 
-def exchange_gather(n, send_count, tile_count, send_rows, tile_row, tile_col, features, tiles):
+def exchange_gather(
+    n, send_count, tile_count, send_rows, tile_row, tile_col, features, tiles, cotangent
+):
     own, edge, width = features.shape
     number = tiles.shape[0]
     slot_count = send_rows.shape[0]
@@ -279,9 +285,11 @@
             jax.ShapeDtypeStruct(table, jnp.int32),
             jax.ShapeDtypeStruct(tiles.shape, bf16),
             jax.ShapeDtypeStruct(features.shape, bf16),
+            jax.ShapeDtypeStruct((own + 1, edge, width), f32),
+            jax.ShapeDtypeStruct(features.shape, bf16),
         ),
-        in_specs=[smem] + [hbm] * 6,
-        out_specs=(vmem,) * 5,
+        in_specs=[smem] + [hbm] * 7,
+        out_specs=(vmem,) * 7,
         scratch_shapes=[
             pltpu.SMEM(send_count.shape, jnp.int32),
             VMEM(send_rows.shape, jnp.int32),
@@ -301,16 +309,18 @@
             dma((number // math.gcd(number, CHUNK),)),
             dma,
             dma((4,)),
+            dma,
         ],
         compiler_params=pltpu.CompilerParams(
-            collective_id=0, has_side_effects=True, vmem_limit_bytes=24 * MIB + slots * 8192
+            collective_id=0, has_side_effects=True,
+            vmem_limit_bytes=min(60 * MIB, 8 * MIB + slots * 40960),
         ),
         name="gather_exchange",
     )(
         tile_count,
         *[
             pltpu.with_memory_space_constraint(a, pltpu.HBM)
-            for a in (send_count, send_rows, tile_row, tile_col, features, tiles)
+            for a in (send_count, send_rows, tile_row, tile_col, features, tiles, cotangent)
         ],
     )
 
@@ -318,13 +328,9 @@
 GROUP = 16
 
 
-def boundary_kernel(table, halo, held, extra):
+def boundary_kernel(table, halo, held, zeros, extra):
     own = extra.shape[0] - 1
     low, high = bits(held.shape[0]), bits(own + halo.shape[0])
-
-    @pl.loop(0, own + 1)
-    def _(r):
-        extra[r] = jnp.zeros(extra.shape[1:], f32)
 
     @pl.loop(0, (table[5, 0] + GROUP - 1) // GROUP)
     def _(g):
@@ -336,17 +342,17 @@
             )
 
 
-def boundary_pass(own, table, halo, held):
-    edge, width = halo.shape[1:]
+def boundary_pass(table, halo, held, zeros):
     vmem = pl.BlockSpec(memory_space=VMEM)
     return pl.pallas_call(
         boundary_kernel,
-        out_shape=jax.ShapeDtypeStruct((own + 1, edge, width), f32),
-        in_specs=[pl.BlockSpec(memory_space=pltpu.SMEM), vmem, vmem],
+        out_shape=jax.ShapeDtypeStruct(zeros.shape, f32),
+        in_specs=[pl.BlockSpec(memory_space=pltpu.SMEM)] + [vmem] * 3,
         out_specs=vmem,
+        input_output_aliases={3: 0},
         compiler_params=pltpu.CompilerParams(vmem_limit_bytes=4 * MIB),
         name="boundary_pass",
-    )(table, halo, held)
+    )(table, halo, held, zeros)
 
 
 SPLIT = 8
@@ -521,12 +527,16 @@
     )(table, held, aggregate, extra, cotangent, weight, bias)
 
 
+def final_step(rows, slots):
+    return math.gcd(rows, 1 << max(9, 19 - bits(slots)))
+
+
 def final_kernel(
     chosen_ref, returned, pieces, bias_sum, own, act, out_hbm, wsum_hbm, bsum_hbm, act_hbm,
     out, wsum, bsum, out_sem, act_sem, small_sem,
 ):
     rows = own.shape[0]
-    step = math.gcd(rows, 512)
+    step = final_step(rows, chosen_ref.shape[1])
     spans = [pl.ds(c * step, step) for c in range(rows // step)]
     wsum[...] = pieces[...].astype(f32)
     bsum[...] = bias_sum[...]
@@ -557,7 +567,7 @@
     rows, width = own_grad.shape
     vmem = pl.BlockSpec(memory_space=VMEM)
     hbm = pl.BlockSpec(memory_space=pltpu.HBM)
-    steps = rows // math.gcd(rows, 512)
+    steps = rows // final_step(rows, returned.shape[0])
     return pl.pallas_call(
         final_kernel,
         out_shape=(
@@ -592,13 +602,14 @@
     slots = n * slot_count
     send_rows = jnp.swapaxes(send_rows, 1, 2).reshape(slot_count, n)
     blocks = lambda a: a.reshape(-1, edge, width)
-    halo, chosen, table, held, aggregate = exchange_gather(
-        n, send_count, tile_count, send_rows, tile_row, tile_col, blocks(features), tile_values
+    halo, chosen, table, held, aggregate, zeros, cotangent = exchange_gather(
+        n, send_count, tile_count, send_rows, tile_row, tile_col, blocks(features), tile_values,
+        blocks(cotangent),
     )
-    extra = boundary_pass(rows // edge, table, blocks(halo), held)
+    extra = boundary_pass(table, blocks(halo), held, zeros)
     scale = float(rows * n) ** (-0.5)
     returned, pieces, bias_sum, own_grad, activation = exchange_return(
-        n, slot_count, scale, table, held, aggregate, extra, blocks(cotangent), weight,
+        n, slot_count, scale, table, held, aggregate, extra, cotangent, weight,
         bias_vector.reshape(1, width),
     )
     grad_features, weight_sum, bias_sum, activation = final_pass(

time: 39.6 us -> 38.5 us (0.972)
  Pallas kernels: 37.7 us -> 36.9 us
    pallas_call x1, Pallas kernels: 1.98 us -> 1.19 us  [boundary_pass(): pl.pallas_call(boundary_kernel, out_shape=jax.ShapeDtypeStruct(zeros.shap...]
    pallas_call x1, Pallas kernels: 2.98 us -> 2.43 us  [final_pass(): pl.pallas_call(final_kernel, out_shape=(jax.ShapeDtypeStruct(own_grad.sha...]
    pallas_call x1, Pallas kernels: 17.2 us -> 17.7 us  [exchange_return(): pl.pallas_call(functools.partial(return_kernel, n, near, slot_count, scal...]
where the time goes in v6:
time: 38.5 us; the launch traced here: 38.2 us
  Pallas kernels  36.9 us (96%)
  between operations  1.33 us (3%)
    pallas_call x1, Pallas kernels, exchange_return(): pl.pallas_call(functools.partial(return_kernel, n, near, slot_count, scal...  17.7 us
    pallas_call x1, Pallas kernels, exchange_gather(): pl.pallas_call(functools.partial(gather_kernel, n), out_shape=(jax.ShapeD...  15.6 us
    pallas_call x1, Pallas kernels, final_pass(): pl.pallas_call(final_kernel, out_shape=(jax.ShapeDtypeStruct(own_grad.sha...  2.43 us
    pallas_call x1, Pallas kernels, boundary_pass(): pl.pallas_call(boundary_kernel, out_shape=jax.ShapeDtypeStruct(zeros.shap...  1.19 us

profile of v6, /device:TPU:0, one launch (start us, length us, event | category | flops | bytes accessed | tf_op | source)
XLA Modules:
  0.0 38.2 jit_solution(13182609677725501919)
XLA Ops:
  1.3 15.6 %gather_exchange.1 = (bf16[32,16,256]{2,1,0:T(8,128)(2,1)S(1)}, s32[1,512]{1,0:T(1,128)S(1)}, s32[8,384]{1,0:T(8,128)S(1)}, bf16[256,128,128]{2,1,0:T(8,128)(2,1...) custom-call(s32[1]{0:T(128)S(6)} %copy.16.tile_count, ...), custom_call_target="tpu_custom_call" | custom-call | tf_op jit(solution)/shard_map/gather_exchange/pallas_call | solution.py:280
  16.9 0.0 copy-start
  16.9 0.0 copy-start.1
  16.9 1.2 %boundary_pass.1.extra = f32[33,128,256]{2,1,0:T(8,128)S(1)} custom-call(s32[8,384]{1,0:T(8,128)S(1)} %get-tuple-element.21.table.table_ref, bf16[4,128,256]{2,1,0:T(8,128)(2,1)S(1)} %bitcast.14, bf16[256,128,128]{2,1,0:T(8,128)(2,1)S(1)} %get-tuple-element.22.held, f32[33,128,256]{2,1,0:T(8,128)S(1)} %get-tuple-element.25.zeros), custom_call_target="tpu_custom_call", output_to_operand_aliasing={{}: (3, {})} | custom-call | tf_op jit(solution)/shard_map/boundary_pass/pallas_call | solution.py:347
  18.1 0.0 copy-done
  18.1 0.0 copy-done.1
  18.1 17.7 %return_exchange.1 = (bf16[32,16,256]{2,1,0:T(8,128)(2,1)S(1)}, bf16[8,32,256]{2,1,0:T(8,128)(2,1)S(1)}, f32[1,256]{1,0:T(1,128)S(1)}, bf16[32,128,256]{2,1,0:T(8,128)(2,1)S(1)}, bf16[32,128,256]{2,1,0:T(8,128)(2,1)S(1)}) custom-call(s32[8,384]{1,0:T(8,128)S(1)} %get-tuple-element.21.table.table_ref, bf16[256,128,128]{2,1,0:T(8,128)(2,1)S(1)} %get-tuple-element.22.held, ...), custom_call_target="tpu_custom_call" | custom-call | tf_op jit(solution)/shard_map/return_exchange/pallas_call | solution.py:490
  35.8 2.4 %final_pass.1 = (bf16[4096,256]{1,0:T(8,128)(2,1)}, f32[256,256]{1,0:T(8,128)}, f32[1,256]{1,0:T(1,128)}, bf16[4096,256]{1,0:T(8,128)(2,1)}) custom-call(s32[1,512]{1,0:T(1,128)S(1)} %get-tuple-element.20.chosen_ref, bf16[512,256]{1,0:T(8,128)(2,1)S(1)} %bitcast.15, bf16[256,256]{1,0:T(8,128)(2,1)S(1)} %bitcast.16, f32[1,256]{1,0:T(1,128)S(1)} %get-tuple-element.29.bias_sum, ...), custom_call_target="tpu_custom_call" | custom-call | tf_op jit(solution)/shard_map/final_pass/pallas_call | solution.py:571
Async XLA Ops:
  16.9 1.2 %copy-start = (bf16[256,256]{1,0:T(8,128)(2,1)S(1)}, bf16[256,256]{1,0:T(8,128)(2,1)}, u32[]{:S(2)}) copy-start(bf16[256,256]{1,0:T(8,128)(2,1)} %weight.1) | copy-start | bytes 393220
  16.9 1.2 %copy-start.1 = (f32[256]{0:T(256)S(1)}, f32[256]{0:T(256)}, u32[]{:S(2)}) copy-start(f32[256]{0:T(256)} %param.12) | copy-start | bytes 3076
